TPU v7x, 256 devices: a 4x2x16 block of a 4x16x16 slice. The times are simulated.
256 devices in a mesh: groups: 2 (over y), row: 16 (over z), col: 4 (over x), ksplit: 2 (over core).
Axes of the slice: x: 4, y: 2, z: 16, core: 2. Of those that a mesh axis runs over, the one named last changes fastest.
The devices are a block of a 4x16x16 slice.
Arguments:
- pair_state: bfloat16 [1024, 512, 128], P(('groups', 'row'), ('col', 'ksplit')), parts along dimension 0, may hold values from -6 to 6
- residue_mask: int32 [1024], P('groups'), parts along dimension 0, may hold values 0 or 1
- input_gain: float32 [128], replicated, may hold values from 0.1 to 1.9
- input_shift: float32 [128], replicated, may hold values from -3 to 3
- left_right: bfloat16 [128, 512], replicated, may hold values from -0.5 to 0.5
- output_gate: bfloat16 [128, 128], replicated, may hold values from -0.5 to 0.5
- final_gain: float32 [128], replicated, may hold values from 0.1 to 1.9
- final_shift: float32 [128], replicated, may hold values from -3 to 3
- output_weight: bfloat16 [128, 128], replicated, may hold values from -0.5 to 0.5
Outputs:
- pair_update: bfloat16 [1024, 512, 128], P(('groups', 'row'), ('col', 'ksplit')), parts along dimension 0
There are 2 independent parts, one for each index of `groups`. A program takes and returns all parts, laid end to end along the dimension named above; an argument that names none is the same for every part. Nothing has to cross between parts.
All inputs are finite; a program needn't handle non-finite values.
Results may differ from a plain program's by a relative error of at most 0.0053.
Values may be sent and summed in bfloat16 or wider, within the bound.
No kernel may reach another device: no remote copies, remote signals or barrier semaphores. Data moves between devices by JAX's collectives and lax.ppermute only.
A program may use at most 64 MiB of HBM per device.

v0:
```python
import jax
import jax.numpy as jnp
from jax import lax
from jax.sharding import PartitionSpec as P


def norm_over(data, norm_gain, norm_shift, over_axis):
    average = jnp.mean(data, axis=over_axis, keepdims=True)
    centred = data - average
    spread = jnp.mean(centred * centred, axis=over_axis, keepdims=True)
    return centred * lax.rsqrt(spread + 1e-05) * norm_gain + norm_shift


def gated_side(normed_in, weights, live_mask, hidden):
    values = jnp.einsum(
        "ikc,ch->hik", normed_in, weights[:, :hidden], preferred_element_type=jnp.float32
    )
    gates = jnp.einsum(
        "ikc,ch->hik", normed_in, weights[:, hidden:], preferred_element_type=jnp.float32
    )
    return (live_mask * jax.nn.sigmoid(gates) * values).astype(jnp.bfloat16)


def contract_parts(left_parts, right_parts, row_count, col_count):
    count_items = left_parts.shape[2]
    tile_rows = left_parts.shape[3]
    tile_cols = left_parts.shape[4]

    def assemble(parts):
        return parts.transpose(2, 0, 3, 1, 4).reshape(
            count_items, row_count * tile_rows, col_count * tile_cols
        )

    products = jnp.einsum(
        "cik,cjk->cij",
        assemble(left_parts),
        assemble(right_parts),
        preferred_element_type=jnp.float32,
    )
    returned = products.reshape(count_items, row_count, tile_rows, col_count, tile_cols)
    return returned.transpose(1, 3, 0, 2, 4)


def body(
    pair_state,
    residue_mask,
    input_gain,
    input_shift,
    left_right,
    output_gate,
    final_gain,
    final_shift,
    output_weight,
):
    tile_rows, tile_cols, channels = pair_state.shape
    hidden = output_weight.shape[0]
    normed_in = norm_over(pair_state.astype(jnp.float32), input_gain, input_shift, 2).astype(
        jnp.bfloat16
    )
    row_start = lax.axis_index("row") * tile_rows
    col_start = lax.axis_index(("col", "ksplit")) * tile_cols
    row_live = lax.dynamic_slice_in_dim(residue_mask, row_start, tile_rows).astype(jnp.float32)
    col_live = lax.dynamic_slice_in_dim(residue_mask, col_start, tile_cols).astype(jnp.float32)
    live_mask = row_live[:, None] * col_live[None, :]
    left_side = gated_side(normed_in, left_right[:, : 2 * hidden], live_mask, hidden)
    right_side = gated_side(normed_in, left_right[:, 2 * hidden :], live_mask, hidden)
    devices_all = lax.axis_size(("row", "col", "ksplit"))
    row_count = lax.axis_size("row")
    col_count = devices_all // row_count
    per_device = hidden // devices_all
    grouped_left = left_side.reshape(devices_all, per_device, tile_rows, tile_cols)
    grouped_right = right_side.reshape(devices_all, per_device, tile_rows, tile_cols)
    left_parts = lax.all_to_all(
        grouped_left, ("row", "col", "ksplit"), split_axis=0, concat_axis=0, tiled=True
    )
    right_parts = lax.all_to_all(
        grouped_right, ("row", "col", "ksplit"), split_axis=0, concat_axis=0, tiled=True
    )
    count_items = left_parts.shape[1]
    shaped_left = left_parts.reshape(row_count, col_count, count_items, tile_rows, tile_cols)
    shaped_right = right_parts.reshape(row_count, col_count, count_items, tile_rows, tile_cols)
    returned = contract_parts(shaped_left, shaped_right, row_count, col_count)
    returned = returned.reshape(devices_all, count_items, tile_rows, tile_cols)
    received = lax.all_to_all(
        returned, ("row", "col", "ksplit"), split_axis=0, concat_axis=0, tiled=True
    )
    mixed_tile = received.reshape(hidden, tile_rows, tile_cols)
    normed_out = norm_over(
        mixed_tile, final_gain[:, None, None], final_shift[:, None, None], 0
    ).astype(jnp.bfloat16)
    projected_out = jnp.einsum(
        "hij,hc->ijc", normed_out, output_weight, preferred_element_type=jnp.float32
    )
    gate_values = jax.nn.sigmoid(
        jnp.einsum("ijc,cd->ijd", normed_in, output_gate, preferred_element_type=jnp.float32)
    )
    return (gate_values * projected_out).astype(jnp.bfloat16)


def solution(mesh):
    placed = (
        P(("groups", "row"), ("col", "ksplit"), None),
        P("groups"),
        P(),
        P(),
        P(),
        P(),
        P(),
        P(),
        P(),
    )
    return jax.shard_map(
        body,
        mesh=mesh,
        in_specs=placed,
        out_specs=P(("groups", "row"), ("col", "ksplit"), None),
        check_vma=False,
    )
```

profile of v0, /device:TPU:33, one launch (start us, length us, event | category | flops | bytes accessed | tf_op | source)
XLA Modules:
  0.0 188.6 jit_solution(7032585861670595083)
XLA Ops:
  0.0 0.8 dynamic-slice_convert_fusion
  0.9 0.8 dynamic-slice_convert_fusion.1
  1.6 1.4 convert_reduce_fusion
  3.0 1.7 fusion.20
  4.8 1.8 fusion.31
  6.6 1.0 fusion.18
  7.6 1.6 copy.18
  9.3 1.4 reshape.110
  10.6 31.0 %all-to-all-start = ((bf16[128,2,1024]{2,1,0:T(2,128)(2,1)}), bf16[128,2,1024]{2,1,0:T(2,128)(2,1)S(1)}, u32[]{:S(2)}, u32[]{:S(2)}) async-start(bf16[128,2,1024]{2,1,0:T(2,128)(2,1)} %reshape.110), calls=%async_computation | async-start | bytes 1048576 | tf_op jit(solution)/shard_map/all_to_all | solution.py:73
  41.7 0.7 fusion.28
  42.4 1.0 fusion.19
  43.4 1.6 copy.20
  45.0 1.4 reshape.108
  46.4 26.0 %all-to-all-done = bf16[128,2,1024]{2,1,0:T(2,128)(2,1)S(1)} async-done(((bf16[128,2,1024]{2,1,0:T(2,128)(2,1)}), bf16[128,2,1024]{2,1,0:T(2,128)(2,1)S(1)}, u32[]{:S(2)}, u32[]{:S(2)}) %all-to-all-start) | async-done | bytes 524320 | tf_op jit(solution)/shard_map/all_to_all | solution.py:73
  72.4 10.1 %all-to-all-start.1 = ((bf16[128,2,1024]{2,1,0:T(2,128)(2,1)}), bf16[128,2,1024]{2,1,0:T(2,128)(2,1)S(1)}, u32[]{:S(2)}, u32[]{:S(2)}) async-start(bf16[128,2,1024]{2,1,0:T(2,128)(2,1)} %reshape.108), calls=%async_computation.1 | async-start | bytes 1048576 | tf_op jit(solution)/shard_map/all_to_all | solution.py:76
  82.5 0.6 reshape.111
  83.1 0.5 copy.19
  83.6 1.4 reshape.103
  85.0 28.3 %all-to-all-done.1 = bf16[128,2,1024]{2,1,0:T(2,128)(2,1)S(1)} async-done(((bf16[128,2,1024]{2,1,0:T(2,128)(2,1)}), bf16[128,2,1024]{2,1,0:T(2,128)(2,1)S(1)}, u32[]{:S(2)}, u32[]{:S(2)}) %all-to-all-start.1) | async-done | bytes 524320 | tf_op jit(solution)/shard_map/all_to_all | solution.py:76
  113.3 0.6 reshape.109
  113.9 0.5 copy.21
  114.3 1.4 reshape.104
  115.8 1.8 fusion.25
  117.5 2.3 %reshape.112 = f32[128,1,2048]{2,1,0:T(1,128)} reshape(f32[128,1,32,64]{3,2,1,0:T(8,128)S(1)} %bitcast.53) | data formatting | bytes 2097152
  119.8 10.2 %all-to-all-start.2 = ((f32[128,1,2048]{2,1,0:T(1,128)}), f32[128,1,2048]{2,1,0:T(1,128)S(1)}, u32[]{:S(2)}, u32[]{:S(2)}) async-start(f32[128,1,2048]{2,1,0:T(1,128)} %reshape.112), calls=%async_computation.2 | async-start | bytes 2097152 | tf_op jit(solution)/shard_map/all_to_all | solution.py:84
  130.0 1.8 fusion.4
  131.8 49.1 %all-to-all-done.2 = f32[128,1,2048]{2,1,0:T(1,128)S(1)} async-done(((f32[128,1,2048]{2,1,0:T(1,128)}), f32[128,1,2048]{2,1,0:T(1,128)S(1)}, u32[]{:S(2)}, u32[]{:S(2)}) %all-to-all-start.2) | async-done | bytes 1048608 | tf_op jit(solution)/shard_map/all_to_all | solution.py:84
  181.0 0.5 broadcast.84
  181.5 3.1 %reduce.1 = f32[128,2048]{1,0:T(8,128)S(1)} reduce(f32[128,1,2048]{2,1,0:T(1,128)S(1)} %all-to-all-done.2, f32[]{:T(128)} %broadcast.84), dimensions={1}, to_apply=%all_to_all.11.reduce_sub_computation | reduce | bytes 2097156 | tf_op jit(solution)/shard_map/all_to_all | solution.py:84
  184.6 0.8 reshape.113
  186.5 0.7 copy-done.3
  187.2 1.3 fusion.15
  (26 shorter events, 1.2 us)
Async XLA Ops:
  0.0 130.0 %copy-start = (bf16[128,128]{1,0:T(8,128)(2,1)S(1)}, bf16[128,128]{1,0:T(8,128)(2,1)}, u32[]{:S(2)}) copy-start(bf16[128,128]{1,0:T(8,128)(2,1)} %param.14) | copy-start | bytes 98308
  0.0 6.6 %copy-start.1 = (bf16[32,64,128]{2,1,0:T(8,128)(2,1)S(1)}, bf16[32,64,128]{2,1,0:T(8,128)(2,1)}, u32[]{:S(2)}) copy-start(bf16[32,64,128]{2,1,0:T(8,128)(2,1)} %param.9) | copy-start | bytes 1572868
  0.0 6.6 %copy-start.7 = (f32[128]{0:T(128)S(1)}, f32[128]{0:T(128)}, u32[]{:S(2)}) copy-start(f32[128]{0:T(128)} %param.11) | copy-start | bytes 1540
  0.0 6.6 %copy-start.6 = (f32[128]{0:T(128)S(1)}, f32[128]{0:T(128)}, u32[]{:S(2)}) copy-start(f32[128]{0:T(128)} %param.12) | copy-start | bytes 1540
  0.0 6.6 %copy-start.4 = (bf16[128,512]{1,0:T(8,128)(2,1)S(1)}, bf16[128,512]{1,0:T(8,128)(2,1)}, u32[]{:S(2)}) copy-start(bf16[128,512]{1,0:T(8,128)(2,1)} %param.13) | copy-start | bytes 393220
  10.6 61.7 %all-to-all-start = ((bf16[128,2,1024]{2,1,0:T(2,128)(2,1)}), bf16[128,2,1024]{2,1,0:T(2,128)(2,1)S(1)}, u32[]{:S(2)}, u32[]{:S(2)}) async-start(bf16[128,2,1024]{2,1,0:T(2,128)(2,1)} %reshape.110), calls=%async_computation | async-start | bytes 1048576 | tf_op jit(solution)/shard_map/all_to_all | solution.py:73
  72.4 40.9 %all-to-all-start.1 = ((bf16[128,2,1024]{2,1,0:T(2,128)(2,1)}), bf16[128,2,1024]{2,1,0:T(2,128)(2,1)S(1)}, u32[]{:S(2)}, u32[]{:S(2)}) async-start(bf16[128,2,1024]{2,1,0:T(2,128)(2,1)} %reshape.108), calls=%async_computation.1 | async-start | bytes 1048576 | tf_op jit(solution)/shard_map/all_to_all | solution.py:76
  113.9 1.9 copy-start.2
  119.8 61.1 %all-to-all-start.2 = ((f32[128,1,2048]{2,1,0:T(1,128)}), f32[128,1,2048]{2,1,0:T(1,128)S(1)}, u32[]{:S(2)}, u32[]{:S(2)}) async-start(f32[128,1,2048]{2,1,0:T(1,128)} %reshape.112), calls=%async_computation.2 | async-start | bytes 2097152 | tf_op jit(solution)/shard_map/all_to_all | solution.py:84
  185.4 0.7 copy-start.8
  185.5 0.7 copy-start.9
  186.0 1.2 copy-start.3
  186.0 1.2 copy-start.5
where the time goes:
time: 191 us; the launch traced here: 189 us
  waiting for transfers between devices  103 us (54%)
  starting transfers between devices  51.3 us (27%)
  local copies, waits for them, and re-layouts  15.4 us (8%)
  matrix products  9.45 us (5%)
  other arithmetic  8.8 us (5%)
    all_to_all x1, waiting for transfers between devices, body(): lax.all_to_all(returned, ('row', 'col', 'ksplit'), split_axis=0, concat_a...  49.1 us
    all_to_all x1, starting transfers between devices, body(): lax.all_to_all(grouped_left, ('row', 'col', 'ksplit'), split_axis=0, conc...  31 us
    all_to_all x1, waiting for transfers between devices, body(): lax.all_to_all(grouped_right, ('row', 'col', 'ksplit'), split_axis=0, con...  28.3 us
    all_to_all x1, waiting for transfers between devices, body(): lax.all_to_all(grouped_left, ('row', 'col', 'ksplit'), split_axis=0, conc...  26 us
    all_to_all x1, starting transfers between devices, body(): lax.all_to_all(returned, ('row', 'col', 'ksplit'), split_axis=0, concat_a...  10.2 us
    all_to_all x1, starting transfers between devices, body(): lax.all_to_all(grouped_right, ('row', 'col', 'ksplit'), split_axis=0, con...  10.1 us
    unnamed x26, local copies, waits for them, and re-layouts  7.94 us
  transfers between devices with their start and end apart: 3, of which 3 were waited for; matrix products, arithmetic and copies ran while one was open for 5% of the time, Pallas kernels for 0%

commit v1 on v0

v1 whole, which is shorter than its diff:
```python
import jax
import jax.numpy as jnp
from jax import lax
from jax.sharding import PartitionSpec as P


def norm_over(data, norm_gain, norm_shift, over_axis):
    average = jnp.mean(data, axis=over_axis, keepdims=True)
    centred = data - average
    spread = jnp.mean(centred * centred, axis=over_axis, keepdims=True)
    return centred * lax.rsqrt(spread + 1e-05) * norm_gain + norm_shift


def gated_side(normed_in, weights, live_mask, hidden):
    values = jnp.einsum(
        "ikc,ch->hik", normed_in, weights[:, :hidden], preferred_element_type=jnp.float32
    )
    gates = jnp.einsum(
        "ikc,ch->hik", normed_in, weights[:, hidden:], preferred_element_type=jnp.float32
    )
    return (live_mask * jax.nn.sigmoid(gates) * values).astype(jnp.bfloat16)


def body(
    pair_state,
    residue_mask,
    input_gain,
    input_shift,
    left_right,
    output_gate,
    final_gain,
    final_shift,
    output_weight,
):
    tile_rows, tile_cols, channels = pair_state.shape
    hidden = output_weight.shape[0]
    every = ("row", "col", "ksplit")
    normed_in = norm_over(pair_state.astype(jnp.float32), input_gain, input_shift, 2).astype(
        jnp.bfloat16
    )
    row_start = lax.axis_index("row") * tile_rows
    col_start = lax.axis_index(("col", "ksplit")) * tile_cols
    row_live = lax.dynamic_slice_in_dim(residue_mask, row_start, tile_rows).astype(jnp.float32)
    col_live = lax.dynamic_slice_in_dim(residue_mask, col_start, tile_cols).astype(jnp.float32)
    live_mask = row_live[:, None] * col_live[None, :]
    left_side = gated_side(normed_in, left_right[:, : 2 * hidden], live_mask, hidden)
    right_side = gated_side(normed_in, left_right[:, 2 * hidden :], live_mask, hidden)
    devices_all = lax.axis_size(every)
    row_count = lax.axis_size("row")
    col_count = devices_all // row_count
    per_device = hidden // devices_all
    both = jnp.concatenate(
        [
            left_side.reshape(devices_all, per_device, tile_rows, tile_cols),
            right_side.reshape(devices_all, per_device, tile_rows, tile_cols),
        ],
        axis=1,
    )
    parts = lax.all_to_all(both, every, split_axis=0, concat_axis=0, tiled=True)
    parts = parts.reshape(row_count, col_count, 2 * per_device, tile_rows, tile_cols)
    whole = parts.transpose(2, 0, 3, 1, 4).reshape(
        2, per_device, row_count * tile_rows, col_count * tile_cols
    )
    products = jnp.einsum(
        "cik,cjk->cij", whole[0], whole[1], preferred_element_type=jnp.float32
    ).astype(jnp.bfloat16)
    returned = products.reshape(per_device, row_count, tile_rows, col_count, tile_cols)
    returned = returned.transpose(1, 3, 0, 2, 4).reshape(
        devices_all, per_device, tile_rows, tile_cols
    )
    received = lax.all_to_all(returned, every, split_axis=0, concat_axis=0, tiled=True)
    mixed_tile = received.reshape(hidden, tile_rows, tile_cols).astype(jnp.float32)
    normed_out = norm_over(
        mixed_tile, final_gain[:, None, None], final_shift[:, None, None], 0
    ).astype(jnp.bfloat16)
    projected_out = jnp.einsum(
        "hij,hc->ijc", normed_out, output_weight, preferred_element_type=jnp.float32
    )
    gate_values = jax.nn.sigmoid(
        jnp.einsum("ijc,cd->ijd", normed_in, output_gate, preferred_element_type=jnp.float32)
    )
    return (gate_values * projected_out).astype(jnp.bfloat16)


def solution(mesh):
    whole = P()
    placed = (P(("groups", "row"), ("col", "ksplit"), None), P("groups")) + (whole,) * 7
    return jax.shard_map(
        body,
        mesh=mesh,
        in_specs=placed,
        out_specs=P(("groups", "row"), ("col", "ksplit"), None),
        check_vma=False,
    )
```

time: 191 us -> 155 us (0.81); the launches traced: 189 us -> 155 us
  blocking collectives: 0 us -> 82.1 us
  waiting for transfers between devices: 103 us -> 30 us
  starting transfers between devices: 51.3 us -> 11.8 us
  matrix products: 9.45 us -> 7.14 us
  other arithmetic: 8.8 us -> 6.88 us
    all_to_all x0 -> x1, blocking collectives: none -> 82.1 us  [body(): parts = lax.all_to_all(both, every, split_axis=0, concat_axis=0, tiled=True)]
    all_to_all x3 -> x1, waiting for transfers between devices: 103 us -> 30 us  [body(): lax.all_to_all(returned, every, split_axis=0, concat_axis=0, tiled=True)]
    all_to_all x3 -> x1, starting transfers between devices: 51.3 us -> 11.8 us  [body(): lax.all_to_all(returned, every, split_axis=0, concat_axis=0, tiled=True)]
    concatenate x0 -> x1, local copies, waits for them, and re-layouts: none -> 3.93 us  [body(): jnp.concatenate([left_side.reshape(devices_all, per_device, tile_rows, ti...]
    all_to_all x1 -> x0, other arithmetic: 3.13 us -> none  [body(): lax.all_to_all(returned, ('row', 'col', 'ksplit'), split_axis=0, concat_a...]
    reshape x2, local copies, waits for them, and re-layouts: 3.24 us -> 0.78 us  [body(): products.reshape(per_device, row_count, tile_rows, col_count, tile_cols)]
    slice x0 -> x3, local copies, waits for them, and re-layouts: none -> 2.3 us  [the longest x2 1.85 us: body(): whole[1]]
    unnamed x26 -> x22, local copies, waits for them, and re-layouts: 7.94 us -> 8.26 us
  transfers between devices with their start and end apart: 3 -> 1, of which waited for: 3 -> 1; matrix products, arithmetic and copies ran while one was open for 5% -> 0% of each run, Pallas kernels for 0% -> 0%
where the time goes in v1:
time: 155 us
  blocking collectives  82.1 us (53%)
  waiting for transfers between devices  30 us (19%)
  local copies, waits for them, and re-layouts  16.5 us (11%)
  starting transfers between devices  11.8 us (8%)
  matrix products  7.14 us (5%)
  other arithmetic  6.88 us (4%)
    all_to_all x1, blocking collectives, body(): parts = lax.all_to_all(both, every, split_axis=0, concat_axis=0, tiled=True)  82.1 us
    all_to_all x1, waiting for transfers between devices, body(): lax.all_to_all(returned, every, split_axis=0, concat_axis=0, tiled=True)  30 us
    all_to_all x1, starting transfers between devices, body(): lax.all_to_all(returned, every, split_axis=0, concat_axis=0, tiled=True)  11.8 us
    unnamed x22, local copies, waits for them, and re-layouts  8.26 us
    concatenate x1, local copies, waits for them, and re-layouts, body(): jnp.concatenate([left_side.reshape(devices_all, per_device, tile_rows, ti...  3.93 us
  transfers between devices with their start and end apart: 1, of which 1 were waited for; matrix products, arithmetic and copies ran while one was open for 0% of the time, Pallas kernels for 0%

profile of v1, /device:TPU:33, one launch (start us, length us, event | category | flops | bytes accessed | tf_op | source)
XLA Modules:
  0.0 154.5 jit_solution(2985661833546629614)
XLA Ops:
  0.0 0.8 dynamic-slice_convert_fusion
  0.9 0.8 dynamic-slice_convert_fusion.1
  1.6 1.4 convert_reduce_fusion.1
  3.0 1.7 %fusion.27 = f32[32,64]{1,0:T(8,128)S(1)} fusion(bf16[32,64,128]{2,1,0:T(8,128)(2,1)} %param.9, f32[32,64]{1,0:T(8,128)S(1)} %broadcast_multiply_fusion.2), kind=kLoop, calls=%fused_computation.36 | loop fusion | flops 1046528 | bytes 540672 | tf_op jit(solution)/shard_map/reduce_sum | solution.py:10
  4.7 0.1 add_rsqrt_fusion.1
  4.8 1.8 %fusion.36 = f32[32,64,128]{2,1,0:T(8,128)S(1)} fusion(bf16[128,512]{1,0:T(8,128)(2,1)} %param.13, bf16[32,64,128]{2,1,0:T(8,128)(2,1)} %param.9, f32[128]{0:T(128)} %param.12, f32[128]{0:T(128)} %param.11, f32[32,64]{1,0:T(8,128)S(1)} %get-tuple-element.7, f32[32,64]{1,0:T(8,128)S(1)} %broadcast_multiply_fusion.2), kind=kOutput, calls=%fused_computation.46 | convolution fusion | flops 68681728 | bytes 1623040 | tf_op jit(solution)/shard_map/ikc,ch->hik/dot_general | solution.py:15
  6.6 0.7 fusion.33
  7.3 1.0 fusion.25
  8.4 1.0 fusion.26
  9.4 1.1 pad_maximum_fusion
  10.5 3.9 %copy.16 = bf16[128,2,32,64]{3,2,1,0:T(8,128)(2,1)S(1)} copy(bf16[128,2,32,64]{0,3,2,1:T(8,128)(2,1)} %pad_maximum_fusion) | data formatting | bytes 2097152 | tf_op jit(solution)/shard_map/concatenate | solution.py:52
  14.4 2.3 %reshape.101 = bf16[128,2,2048]{2,1,0:T(2,128)(2,1)} reshape(bf16[128,2,32,64]{3,2,1,0:T(8,128)(2,1)S(1)} %copy.16) | data formatting | bytes 2097152
  16.7 82.1 %all_to_all.10 = bf16[128,2,2048]{2,1,0:T(2,128)(2,1)} all-to-all(bf16[128,2,2048]{2,1,0:T(2,128)(2,1)} %reshape.101), channel_id=1, replica_groups=mesh['groups'=2,'row'=16,'col'=4,'ksplit'=2] {'row','col','ksplit'}, dimensions={0} | all-to-all | bytes 2097152 | tf_op jit(solution)/shard_map/all_to_all | solution.py:59
  98.8 3.8 %reshape.102 = bf16[128,2,32,64]{3,2,1,0:T(8,128)(2,1)S(1)} reshape(bf16[128,2,2048]{2,1,0:T(2,128)(2,1)} %all_to_all.10) | data formatting | bytes 2097152
  102.6 1.4 fusion.49
  104.0 0.5 copy.17
  104.4 0.6 reshape.91
  105.0 0.2 copy-done.2
  105.2 0.5 copy.18
  105.6 0.6 reshape.92
  106.3 0.5 convolution_convert_fusion
  106.7 0.5 reshape.93
  107.3 0.2 copy.19
  107.5 1.4 reshape.103
  108.9 11.8 %all-to-all-start.1 = ((bf16[128,2,1024]{2,1,0:T(2,128)(2,1)}), bf16[128,2,1024]{2,1,0:T(2,128)(2,1)S(1)}, u32[]{:S(2)}, u32[]{:S(2)}) async-start(bf16[128,2,1024]{2,1,0:T(2,128)(2,1)} %reshape.103), calls=%async_computation.1 | async-start | bytes 1048576 | tf_op jit(solution)/shard_map/all_to_all | solution.py:71
  120.7 0.7 fusion.11
  121.5 30.0 %all-to-all-done.1 = bf16[128,2,1024]{2,1,0:T(2,128)(2,1)S(1)} async-done(((bf16[128,2,1024]{2,1,0:T(2,128)(2,1)}), bf16[128,2,1024]{2,1,0:T(2,128)(2,1)S(1)}, u32[]{:S(2)}, u32[]{:S(2)}) %all-to-all-start.1) | async-done | bytes 524320 | tf_op jit(solution)/shard_map/all_to_all | solution.py:71
  151.4 0.6 reshape.104
  152.0 0.3 convert_reduce_fusion
  152.3 0.4 fusion.3
  152.7 0.4 fusion.6
  153.2 1.4 fusion.22
  (20 shorter events, 0.1 us)
Async XLA Ops:
  0.0 120.7 %copy-start = (bf16[128,128]{1,0:T(8,128)(2,1)S(1)}, bf16[128,128]{1,0:T(8,128)(2,1)}, u32[]{:S(2)}) copy-start(bf16[128,128]{1,0:T(8,128)(2,1)} %param.14) | copy-start | bytes 98308
  0.0 6.6 %copy-start.1 = (bf16[32,64,128]{2,1,0:T(8,128)(2,1)S(1)}, bf16[32,64,128]{2,1,0:T(8,128)(2,1)}, u32[]{:S(2)}) copy-start(bf16[32,64,128]{2,1,0:T(8,128)(2,1)} %param.9) | copy-start | bytes 1572868
  0.0 6.6 %copy-start.6 = (f32[128]{0:T(128)S(1)}, f32[128]{0:T(128)}, u32[]{:S(2)}) copy-start(f32[128]{0:T(128)} %param.11) | copy-start | bytes 1540
  0.0 6.6 %copy-start.5 = (f32[128]{0:T(128)S(1)}, f32[128]{0:T(128)}, u32[]{:S(2)}) copy-start(f32[128]{0:T(128)} %param.12) | copy-start | bytes 1540
  0.0 6.6 %copy-start.3 = (bf16[128,512]{1,0:T(8,128)(2,1)S(1)}, bf16[128,512]{1,0:T(8,128)(2,1)}, u32[]{:S(2)}) copy-start(bf16[128,512]{1,0:T(8,128)(2,1)} %param.13) | copy-start | bytes 393220
  104.0 1.2 copy-start.2
  108.9 42.5 %all-to-all-start.1 = ((bf16[128,2,1024]{2,1,0:T(2,128)(2,1)}), bf16[128,2,1024]{2,1,0:T(2,128)(2,1)S(1)}, u32[]{:S(2)}, u32[]{:S(2)}) async-start(bf16[128,2,1024]{2,1,0:T(2,128)(2,1)} %reshape.103), calls=%async_computation.1 | async-start | bytes 1048576 | tf_op jit(solution)/shard_map/all_to_all | solution.py:71
  121.4 31.3 %copy-start.7 = (f32[128]{0:T(128)S(1)}, f32[128]{0:T(128)}, u32[]{:S(2)}) copy-start(f32[128]{0:T(128)} %param.16) | copy-start | bytes 1540
  121.5 31.3 %copy-start.8 = (f32[128]{0:T(128)S(1)}, f32[128]{0:T(128)}, u32[]{:S(2)}) copy-start(f32[128]{0:T(128)} %param.15) | copy-start | bytes 1540
  152.0 1.1 copy-start.4

commit v2 on v1

v2 whole, which is shorter than its diff:
```python
import jax, functools
import jax.numpy as jnp
from jax import lax
from jax.experimental import pallas as pl
from jax.experimental.pallas import tpu as pltpu
F32=jnp.float32; BF16=jnp.bfloat16

def prologue_kernel(where_ref, live_ref, cols_ref, x_ref, gain_ref, shift_ref, wl_ref, wr_ref, both_ref, normed_ref):
    rows, cols, chans = x_ref.shape
    half = rows // 2
    hidden = wl_ref.shape[0] // 2
    lanes = 2 * cols
    low = lax.broadcasted_iota(jnp.int32, (1, lanes), 1) < cols
    vec = cols_ref[pl.ds(where_ref[1] // lanes, 1), :]
    turned = pltpu.roll(vec, cols, 1)
    first = (where_ref[1] % lanes) == 0
    col_live = jnp.where(low == first, vec, turned)
    step = 8
    for base in range(0, half, step):
        parts = []
        for start in (base, base + half):
            data = x_ref[start:start + step].astype(F32)
            average = jnp.mean(data, axis=-1, keepdims=True)
            centred = data - average
            spread = jnp.mean(centred * centred, axis=-1, keepdims=True)
            normed = (centred * lax.rsqrt(spread + 1e-05) * gain_ref[...] + shift_ref[...]).astype(BF16)
            normed_ref[start:start + step] = normed
            parts.append(normed)
        top, bottom = parts
        straight = jnp.stack([top, bottom], axis=1).reshape(step * lanes, chans)
        crossed = jnp.stack([bottom, top], axis=1).reshape(step * lanes, chans)
        nt = (((1,), (1,)), ((), ()))
        left = lax.dot_general(wl_ref[...], straight, nt, preferred_element_type=F32)
        right = lax.dot_general(wr_ref[...], crossed, nt, preferred_element_type=F32)
        left = left[:hidden] * jax.nn.sigmoid(left[hidden:])
        right = right[:hidden] * jax.nn.sigmoid(right[hidden:])
        upper, lower = [], []
        for t in range(step):
            m_top = live_ref[where_ref[0] + base + t].astype(F32)
            m_bot = live_ref[where_ref[0] + base + half + t].astype(F32)
            lt = left[:, t * lanes:(t + 1) * lanes] * (jnp.where(low, m_top, m_bot) * col_live)
            rt = right[:, t * lanes:(t + 1) * lanes] * (jnp.where(low, m_bot, m_top) * col_live)
            upper.append(jnp.where(low, lt, rt))
            lower.append(jnp.where(low, rt, lt))
        both_ref[:, base:base + step, :] = jnp.swapaxes(jnp.stack(upper, axis=0), 0, 1).astype(BF16)
        both_ref[:, base + half:base + half + step, :] = jnp.swapaxes(jnp.stack(lower, axis=0), 0, 1).astype(BF16)

def middle_kernel(in_ref, out_ref):
    nrow, ncol, rows, lanes = in_ref.shape
    half = rows // 2
    cols = lanes // 2
    low = lax.broadcasted_iota(jnp.int32, (1, 1, lanes), 2) < cols
    def sides(k):
        a = in_ref[:, k, :half].astype(F32); b = in_ref[:, k, half:].astype(F32)
        ar = pltpu.roll(a, cols, 2); br = pltpu.roll(b, cols, 2)
        lr = jnp.concatenate([a, br], axis=1); rl = jnp.concatenate([ar, b], axis=1)
        return lr, rl
    lefts, rights = [], []
    for k in range(0, ncol, 2):
        lr0, rl0 = sides(k); lr1, rl1 = sides(k + 1)
        lefts.append(jnp.where(low, lr0, rl1).astype(BF16).reshape(nrow * rows, lanes))
        rights.append(jnp.where(low, rl0, lr1).astype(BF16).reshape(nrow * rows, lanes))
    left = jnp.concatenate(lefts, axis=1); right = jnp.concatenate(rights, axis=1)
    product = lax.dot_general(left, right, (((1,), (1,)), ((), ())), preferred_element_type=F32)
    for k in range(0, ncol, 2):
        tile = product[:, k * cols:(k + 2) * cols].reshape(nrow, rows, lanes)
        a = tile[:, :half]; b = tile[:, half:]
        ar = pltpu.roll(a, cols, 2); br = pltpu.roll(b, cols, 2)
        out_ref[:, k] = jnp.where(low, a, br).astype(BF16)
        out_ref[:, k + 1] = jnp.where(low, ar, b).astype(BF16)

def prologue(x, residue_mask, gain, shift, weights, row_start, col_start):
    rows, cols, chans = x.shape
    hidden = weights.shape[1] // 4
    place = jnp.stack([row_start, col_start]).astype(jnp.int32)
    wt = weights.T
    smem = pl.BlockSpec(memory_space=pltpu.SMEM); vmem = pl.BlockSpec(memory_space=pltpu.VMEM)
    return pl.pallas_call(
        prologue_kernel,
        out_shape=(jax.ShapeDtypeStruct((hidden, rows, 2 * cols), BF16), jax.ShapeDtypeStruct((rows, cols, chans), BF16)),
        in_specs=[smem, smem] + [vmem] * 6,
        out_specs=(vmem, vmem),
        name="prologue",
    )(place, residue_mask, residue_mask.astype(F32).reshape(-1, 2 * cols), x, gain.reshape(1, 1, -1), shift.reshape(1, 1, -1), wt[: 2 * hidden], wt[2 * hidden :])

def middle(parts, row_count, col_count):
    n, rows, lanes = parts.shape
    vmem = pl.BlockSpec(memory_space=pltpu.VMEM)
    out = pl.pallas_call(
        middle_kernel,
        out_shape=jax.ShapeDtypeStruct((row_count, col_count, rows // 2, lanes), BF16),
        in_specs=[vmem], out_specs=vmem, name="middle",
    )(parts.reshape(row_count, col_count, rows, lanes))
    return out.reshape(n, rows // 2, lanes)

from jax.sharding import PartitionSpec as P


def body(
    pair_state,
    residue_mask,
    input_gain,
    input_shift,
    left_right,
    output_gate,
    final_gain,
    final_shift,
    output_weight,
):
    tile_rows, tile_cols, channels = pair_state.shape
    hidden = output_weight.shape[0]
    every = ("row", "col", "ksplit")
    row_start = lax.axis_index("row") * tile_rows
    col_start = lax.axis_index(("col", "ksplit")) * tile_cols
    row_count = lax.axis_size("row")
    col_count = lax.axis_size(("col", "ksplit"))
    both, normed_in = prologue(
        pair_state, residue_mask, input_gain, input_shift, left_right, row_start, col_start
    )
    parts = lax.all_to_all(both, every, split_axis=0, concat_axis=0, tiled=True)
    returned = middle(parts, row_count, col_count)
    received = lax.all_to_all(returned, every, split_axis=0, concat_axis=0, tiled=True)
    mixed = received.astype(F32)
    average = jnp.mean(mixed, axis=0, keepdims=True)
    centred = mixed - average
    spread = jnp.mean(centred * centred, axis=0, keepdims=True)
    normed_out = (
        centred * lax.rsqrt(spread + 1e-05) * final_gain[:, None, None]
        + final_shift[:, None, None]
    ).astype(BF16)
    projected_out = jnp.einsum(
        "hrl,hc->rlc", normed_out, output_weight, preferred_element_type=F32
    )
    projected_out = projected_out.reshape(tile_rows // 2, 2, tile_cols, channels)
    projected_out = projected_out.transpose(1, 0, 2, 3).reshape(tile_rows, tile_cols, channels)
    gate_values = jax.nn.sigmoid(
        jnp.einsum("ijc,cd->ijd", normed_in, output_gate, preferred_element_type=F32)
    )
    return (gate_values * projected_out).astype(BF16)


def solution(mesh):
    whole = P()
    placed = (P(("groups", "row"), ("col", "ksplit"), None), P("groups")) + (whole,) * 7
    return jax.shard_map(
        body,
        mesh=mesh,
        in_specs=placed,
        out_specs=P(("groups", "row"), ("col", "ksplit"), None),
        check_vma=False,
    )
```

time: 155 us -> 139 us (0.90)
  blocking collectives: 82.1 us -> 125 us
  waiting for transfers between devices: 30 us -> 0 us
  local copies, waits for them, and re-layouts: 16.5 us -> 4.04 us
  starting transfers between devices: 11.8 us -> 0 us
  Pallas kernels: 0 us -> 6.45 us
  matrix products: 7.14 us -> 1.55 us
  other arithmetic: 6.88 us -> 1.83 us
    all_to_all x0 -> x1, blocking collectives: none -> 42.5 us  [body(): lax.all_to_all(returned, every, split_axis=0, concat_axis=0, tiled=True)]
    all_to_all x1 -> x0, waiting for transfers between devices: 30 us -> none  [body(): lax.all_to_all(returned, every, split_axis=0, concat_axis=0, tiled=True)]
    all_to_all x1 -> x0, starting transfers between devices: 11.8 us -> none  [body(): lax.all_to_all(returned, every, split_axis=0, concat_axis=0, tiled=True)]
    pallas_call x0 -> x2, Pallas kernels: none -> 6.45 us  [the longest x1 3.66 us: prologue(): pl.pallas_call(prologue_kernel, out_shape=(jax.ShapeDtypeStruct((hidden,...]
    dot_general x6 -> x1, matrix products: 6.39 us -> 0.33 us  [body(): jnp.einsum('hrl,hc->rlc', normed_out, output_weight, preferred_element_ty...]
    unnamed x22 -> x13, local copies, waits for them, and re-layouts: 8.26 us -> 3.28 us
    concatenate x1 -> x0, local copies, waits for them, and re-layouts: 3.93 us -> none  [body(): jnp.concatenate([left_side.reshape(devices_all, per_device, tile_rows, ti...]
    reduce_sum x4 -> x2, other arithmetic: 3.71 us -> 0.32 us  [the longest x1 0.18 us: body(): spread = jnp.mean(centred * centred, axis=0, keepdims=True)]
  transfers between devices with their start and end apart: 1 -> 0, of which waited for: 1 -> 0; matrix products, arithmetic and copies ran while one was open for 0% -> 0% of each run, Pallas kernels for 0% -> 0%
where the time goes in v2:
time: 139 us
  blocking collectives  125 us (90%)
  Pallas kernels  6.45 us (5%)
  local copies, waits for them, and re-layouts  4.04 us (3%)
  other arithmetic  1.83 us (1%)
  matrix products  1.55 us (1%)
    all_to_all x1, blocking collectives, body(): parts = lax.all_to_all(both, every, split_axis=0, concat_axis=0, tiled=True)  82.1 us
    all_to_all x1, blocking collectives, body(): lax.all_to_all(returned, every, split_axis=0, concat_axis=0, tiled=True)  42.5 us
    pallas_call x1, Pallas kernels, prologue(): pl.pallas_call(prologue_kernel, out_shape=(jax.ShapeDtypeStruct((hidden,...  3.66 us
    unnamed x13, local copies, waits for them, and re-layouts  3.28 us
    pallas_call x1, Pallas kernels, middle(): pl.pallas_call(middle_kernel, out_shape=jax.ShapeDtypeStruct((row_count,...  2.8 us

profile of v2, /device:TPU:33, one launch (start us, length us, event | category | flops | bytes accessed | tf_op | source)
XLA Modules:
  0.0 138.5 jit_solution(1677339165218455826)
XLA Ops:
  0.0 0.0 copy-start
  0.0 0.0 copy-start.1
  0.0 0.7 copy-done.1
  0.7 0.6 convert_bitcast_fusion.cols_ref
  1.3 1.0 copy.13
  2.3 0.7 fusion.15
  3.0 0.6 pad_add_fusion.where_ref
  3.5 3.7 %prologue.1 = (bf16[128,32,128]{2,1,0:T(8,128)(2,1)}, bf16[32,64,128]{2,1,0:T(8,128)(2,1)}) custom-call(s32[2]{0:T(128)} %pad_add_fusion.where_ref, s32[512]{0:T(512)} %live_ref.1, f32[4,128]{1,0:T(4,128)} %convert_bitcast_fusion.cols_ref, bf16[32,64,128]{2,1,0:T(8,128)(2,1)} %x_ref.1, f32[1,1,128]{2,1,0:T(1,128)} %bitcast.25, f32[1,1,128]{2,1,0:T(1,128)} %bitcast.26, ...), custom_call_target="tpu_custom_call" | custom-call | tf_op jit(solution)/shard_map/prologue/pallas_call | solution.py:78
  7.2 82.1 %all_to_all.10 = bf16[128,32,128]{2,1,0:T(8,128)(2,1)} all-to-all(bf16[128,32,128]{2,1,0:T(8,128)(2,1)} %get-tuple-element.8), channel_id=1, replica_groups=mesh['groups'=2,'row'=16,'col'=4,'ksplit'=2] {'row','col','ksplit'}, dimensions={0} | all-to-all | bytes 2097152 | tf_op jit(solution)/shard_map/all_to_all | solution.py:120
  89.3 2.8 %middle.1 = bf16[16,8,16,128]{3,2,1,0:T(8,128)(2,1)} custom-call(bf16[16,8,32,128]{3,2,1,0:T(8,128)(2,1)} %bitcast.20), custom_call_target="tpu_custom_call" | custom-call | tf_op jit(solution)/shard_map/middle/pallas_call | solution.py:89
  92.1 42.5 %all_to_all.11 = bf16[128,16,128]{2,1,0:T(8,128)(2,1)S(1)} all-to-all(bf16[128,16,128]{2,1,0:T(8,128)(2,1)} %bitcast.22), channel_id=1, replica_groups=mesh['groups'=2,'row'=16,'col'=4,'ksplit'=2] {'row','col','ksplit'}, dimensions={0} | all-to-all | bytes 1048576 | tf_op jit(solution)/shard_map/all_to_all | solution.py:122
  134.6 0.1 convert_reduce_fusion
  134.7 0.2 fusion.7
  134.9 0.0 copy-start.2
  134.9 0.0 copy-start.3
  134.9 0.6 copy-done.2
  135.6 0.0 copy-done.3
  135.6 0.3 fusion.10
  135.9 0.0 copy-done
  135.9 0.3 fusion.11
  136.3 0.0 copy-start.4
  136.3 0.0 copy-start.5
  136.3 0.1 copy.15
  136.4 0.9 copy-done.4
  137.3 0.0 copy-done.5
  137.3 1.2 fusion.4
  (2 shorter events, 0.0 us)
Async XLA Ops:
  0.0 135.9 %copy-start = (bf16[128,128]{1,0:T(8,128)(2,1)S(1)}, bf16[128,128]{1,0:T(8,128)(2,1)}, u32[]{:S(2)}) copy-start(bf16[128,128]{1,0:T(8,128)(2,1)} %param.17) | copy-start | bytes 98308
  0.0 0.7 copy-start.1
  134.9 0.7 copy-start.2
  134.9 0.7 copy-start.3
  136.3 1.0 copy-start.4
  136.3 1.0 copy-start.5

commit v3 on v2

v3 whole, which is shorter than its diff:
```python
import jax
import jax.numpy as jnp
from jax import lax
from jax.experimental import pallas as pl
from jax.experimental.pallas import tpu as pltpu
from jax.sharding import PartitionSpec as P

F32 = jnp.float32
BF16 = jnp.bfloat16
ACROSS = (((1,), (1,)), ((), ()))


def norm_rows(data, norm_gain, norm_shift):
    average = jnp.mean(data, axis=-1, keepdims=True)
    centred = data - average
    spread = jnp.mean(centred * centred, axis=-1, keepdims=True)
    return (centred * lax.rsqrt(spread + 1e-05) * norm_gain + norm_shift).astype(BF16)


def prologue_kernel(live_ref, cols_ref, x_ref, gain_ref, shift_ref, weights_ref, both_ref):
    _, step, cols, chans = x_ref.shape
    hidden = weights_ref.shape[1] // 4
    lanes = 2 * cols
    half = step * pl.num_programs(0)
    row_start = lax.axis_index("row") * (2 * half) + pl.program_id(0) * step
    col_index = lax.axis_index("col") * lax.axis_size("ksplit") + lax.axis_index("ksplit")
    low = lax.broadcasted_iota(jnp.int32, (1, lanes), 1) < cols
    pair = cols_ref[pl.ds(col_index // 2, 1), :].astype(F32)
    swapped = pltpu.roll(pair, cols, 1)
    own_low = jnp.where(low, pair, swapped)
    own_high = jnp.where(low, swapped, pair)
    odd = (col_index % 2).astype(F32)
    col_live = own_high * odd + own_low * (1.0 - odd)
    top = norm_rows(x_ref[0].astype(F32), gain_ref[...], shift_ref[...])
    bottom = norm_rows(x_ref[1].astype(F32), gain_ref[...], shift_ref[...])
    straight = jnp.stack([top, bottom], axis=1).reshape(step * lanes, chans)
    crossed = jnp.stack([bottom, top], axis=1).reshape(step * lanes, chans)
    turned = weights_ref[...].T
    left = lax.dot_general(turned[: 2 * hidden], straight, ACROSS, preferred_element_type=F32)
    right = lax.dot_general(turned[2 * hidden :], crossed, ACROSS, preferred_element_type=F32)
    left = left[:hidden] * jax.nn.sigmoid(left[hidden:])
    right = right[:hidden] * jax.nn.sigmoid(right[hidden:])
    upper, lower = [], []
    for t in range(step):
        live_top = live_ref[row_start + t].astype(F32)
        live_bottom = live_ref[row_start + half + t].astype(F32)
        span = slice(t * lanes, (t + 1) * lanes)
        from_left = left[:, span] * (jnp.where(low, live_top, live_bottom) * col_live)
        from_right = right[:, span] * (jnp.where(low, live_bottom, live_top) * col_live)
        upper.append(jnp.where(low, from_left, from_right))
        lower.append(jnp.where(low, from_right, from_left))
    both_ref[:, 0] = jnp.swapaxes(jnp.stack(upper, axis=0), 0, 1).astype(BF16)
    both_ref[:, 1] = jnp.swapaxes(jnp.stack(lower, axis=0), 0, 1).astype(BF16)


def prologue(pair_state, residue_mask, input_gain, input_shift, left_right):
    rows, cols, chans = pair_state.shape
    hidden = left_right.shape[1] // 4
    half = rows // 2
    step = 8
    lanes = 2 * cols
    still = lambda s: (0, 0)
    both = pl.pallas_call(
        prologue_kernel,
        grid=(half // step,),
        out_shape=jax.ShapeDtypeStruct((hidden, 2, half, lanes), BF16),
        in_specs=[
            pl.BlockSpec(memory_space=pltpu.SMEM),
            pl.BlockSpec((residue_mask.shape[0] // lanes, lanes), still),
            pl.BlockSpec((2, step, cols, chans), lambda s: (0, s, 0, 0)),
            pl.BlockSpec((1, chans), still),
            pl.BlockSpec((1, chans), still),
            pl.BlockSpec((chans, 4 * hidden), still),
        ],
        out_specs=pl.BlockSpec((hidden, 2, step, lanes), lambda s: (0, 0, s, 0)),
        name="prologue",
    )(
        residue_mask,
        residue_mask.reshape(-1, lanes),
        pair_state.reshape(2, half, cols, chans),
        input_gain.reshape(1, -1),
        input_shift.reshape(1, -1),
        left_right,
    )
    return both.reshape(hidden, rows, lanes)


def gate_kernel(x_ref, gain_ref, shift_ref, weights_ref, gate_ref):
    _, rows, cols, chans = x_ref.shape
    normed = norm_rows(x_ref[...].astype(F32), gain_ref[...], shift_ref[...])
    raised = jnp.dot(
        normed.reshape(2 * rows * cols, chans), weights_ref[...], preferred_element_type=F32
    )
    gated = jax.nn.sigmoid(raised).reshape(2, rows, cols, chans)
    gate_ref[:, 0] = gated[0]
    gate_ref[:, 1] = gated[1]


def output_gates(pair_state, input_gain, input_shift, output_gate):
    rows, cols, chans = pair_state.shape
    half = rows // 2
    step = 8
    still = lambda s: (0, 0)
    return pl.pallas_call(
        gate_kernel,
        grid=(half // step,),
        out_shape=jax.ShapeDtypeStruct((half, 2, cols, chans), F32),
        in_specs=[
            pl.BlockSpec((2, step, cols, chans), lambda s: (0, s, 0, 0)),
            pl.BlockSpec((1, chans), still),
            pl.BlockSpec((1, chans), still),
            pl.BlockSpec((chans, chans), still),
        ],
        out_specs=pl.BlockSpec((step, 2, cols, chans), lambda s: (s, 0, 0, 0)),
        cost_estimate=pl.CostEstimate(
            flops=2 * rows * cols * chans * chans,
            bytes_accessed=6 * rows * cols * chans,
            transcendentals=rows * cols * chans,
        ),
        name="output_gates",
    )(
        pair_state.reshape(2, half, cols, chans),
        input_gain.reshape(1, -1),
        input_shift.reshape(1, -1),
        output_gate,
    )


def middle_kernel(in_ref, out_ref):
    nrow, ncol, rows, lanes = in_ref.shape
    half = rows // 2
    cols = lanes // 2
    low = lax.broadcasted_iota(jnp.int32, (1, 1, lanes), 2) < cols

    def sides(k):
        top = in_ref[:, k, :half].astype(F32)
        bottom = in_ref[:, k, half:].astype(F32)
        straight = jnp.concatenate([top, pltpu.roll(bottom, cols, 2)], axis=1)
        crossed = jnp.concatenate([pltpu.roll(top, cols, 2), bottom], axis=1)
        return straight, crossed

    lefts, rights = [], []
    for k in range(0, ncol, 2):
        straight, crossed = sides(k)
        straight_next, crossed_next = sides(k + 1)
        left = jnp.where(low, straight, crossed_next).astype(BF16)
        right = jnp.where(low, crossed, straight_next).astype(BF16)
        lefts.append(left.reshape(nrow * rows, lanes))
        rights.append(right.reshape(nrow * rows, lanes))
    product = lax.dot_general(
        jnp.concatenate(lefts, axis=1),
        jnp.concatenate(rights, axis=1),
        ACROSS,
        preferred_element_type=F32,
    )
    for k in range(0, ncol, 2):
        tile = product[:, k * cols : (k + 2) * cols].reshape(nrow, rows, lanes)
        top = tile[:, :half]
        bottom = tile[:, half:]
        out_ref[:, k] = jnp.where(low, top, pltpu.roll(bottom, cols, 2)).astype(BF16)
        out_ref[:, k + 1] = jnp.where(low, pltpu.roll(top, cols, 2), bottom).astype(BF16)


def middle(parts, row_count, col_count):
    count, rows, lanes = parts.shape
    vmem = pl.BlockSpec(memory_space=pltpu.VMEM)
    returned = pl.pallas_call(
        middle_kernel,
        out_shape=jax.ShapeDtypeStruct((row_count, col_count, rows // 2, lanes), BF16),
        in_specs=[vmem],
        out_specs=vmem,
        name="middle",
    )(parts.reshape(row_count, col_count, rows, lanes))
    return returned.reshape(count, rows // 2, lanes)


def body(
    pair_state,
    residue_mask,
    input_gain,
    input_shift,
    left_right,
    output_gate,
    final_gain,
    final_shift,
    output_weight,
):
    tile_rows, tile_cols, channels = pair_state.shape
    every = ("row", "col", "ksplit")
    row_count = lax.axis_size("row")
    col_count = lax.axis_size(("col", "ksplit"))
    both = prologue(pair_state, residue_mask, input_gain, input_shift, left_right)
    gates = output_gates(pair_state, input_gain, input_shift, output_gate)
    parts = lax.all_to_all(both, every, split_axis=0, concat_axis=0, tiled=True)
    returned = middle(parts, row_count, col_count)
    received = lax.all_to_all(returned, every, split_axis=0, concat_axis=0, tiled=True)
    mixed = received.astype(F32)
    average = jnp.mean(mixed, axis=0, keepdims=True)
    centred = mixed - average
    spread = jnp.mean(centred * centred, axis=0, keepdims=True)
    normed_out = (
        centred * lax.rsqrt(spread + 1e-05) * final_gain[:, None, None]
        + final_shift[:, None, None]
    ).astype(BF16)
    projected_out = jnp.einsum(
        "hrl,hc->rlc", normed_out, output_weight, preferred_element_type=F32
    )
    update = gates * projected_out.reshape(tile_rows // 2, 2, tile_cols, channels)
    update = update.transpose(1, 0, 2, 3).astype(BF16)
    return update.reshape(tile_rows, tile_cols, channels)


def solution(mesh):
    whole = P()
    placed = (P(("groups", "row"), ("col", "ksplit"), None), P("groups")) + (whole,) * 7
    return jax.shard_map(
        body,
        mesh=mesh,
        in_specs=placed,
        out_specs=P(("groups", "row"), ("col", "ksplit"), None),
        check_vma=False,
    )
```

time: 139 us -> 135 us (0.971)
  blocking collectives: 125 us -> 82.1 us
  waiting for transfers between devices: 0 us -> 28 us
  starting transfers between devices: 0 us -> 11.8 us
  Pallas kernels: 6.45 us -> 9.56 us
  local copies, waits for them, and re-layouts: 4.04 us -> 2.36 us
    all_to_all x1 -> x0, blocking collectives: 42.5 us -> none  [body(): lax.all_to_all(returned, every, split_axis=0, concat_axis=0, tiled=True)]
    all_to_all x0 -> x1, waiting for transfers between devices: none -> 28 us  [body(): lax.all_to_all(returned, every, split_axis=0, concat_axis=0, tiled=True)]
    all_to_all x0 -> x1, starting transfers between devices: none -> 11.8 us  [body(): lax.all_to_all(returned, every, split_axis=0, concat_axis=0, tiled=True)]
    pallas_call x1 -> x2, Pallas kernels: 3.66 us -> 6.77 us  [the longest x1 4 us: prologue(): pl.pallas_call(prologue_kernel, grid=(half // step,), out_shape=jax.Shape...]
    unnamed x13 -> x8, local copies, waits for them, and re-layouts: 3.28 us -> 1.53 us
  transfers between devices with their start and end apart: 0 -> 1, of which waited for: 0 -> 1; matrix products, arithmetic and copies ran while one was open for 0% -> 0% of each run, Pallas kernels for 0% -> 2%
where the time goes in v3:
time: 135 us
  blocking collectives  82.1 us (61%)
  waiting for transfers between devices  28 us (21%)
  starting transfers between devices  11.8 us (9%)
  Pallas kernels  9.56 us (7%)
  local copies, waits for them, and re-layouts  2.36 us (2%)
    all_to_all x1, blocking collectives, body(): parts = lax.all_to_all(both, every, split_axis=0, concat_axis=0, tiled=True)  82.1 us
    all_to_all x1, waiting for transfers between devices, body(): lax.all_to_all(returned, every, split_axis=0, concat_axis=0, tiled=True)  28 us
    all_to_all x1, starting transfers between devices, body(): lax.all_to_all(returned, every, split_axis=0, concat_axis=0, tiled=True)  11.8 us
    pallas_call x1, Pallas kernels, prologue(): pl.pallas_call(prologue_kernel, grid=(half // step,), out_shape=jax.Shape...  4 us
    pallas_call x1, Pallas kernels, middle(): pl.pallas_call(middle_kernel, out_shape=jax.ShapeDtypeStruct((row_count,...  2.79 us
    pallas_call x1, Pallas kernels, output_gates(): pl.pallas_call(gate_kernel, grid=(half // step,), out_shape=jax.ShapeDtyp...  2.77 us
  transfers between devices with their start and end apart: 1, of which 1 were waited for; matrix products, arithmetic and copies ran while one was open for 0% of the time, Pallas kernels for 2%

profile of v3, /device:TPU:33, one launch (start us, length us, event | category | flops | bytes accessed | tf_op | source)
XLA Modules:
  0.0 135.0 jit_solution(2896375064021342259)
XLA Ops:
  0.0 0.0 copy-start
  0.0 4.0 %prologue.1 = bf16[128,2,16,128]{3,2,1,0:T(8,128)(2,1)} custom-call(s32[512]{0:T(512)} %live_ref.1, s32[4,128]{1,0:T(4,128)} %bitcast.20, bf16[2,16,64,128]{3,2,1,0:T(8,128)(2,1)} %bitcast.18, f32[1,128]{1,0:T(1,128)} %bitcast.21, f32[1,128]{1,0:T(1,128)} %bitcast.23, bf16[128,512]{1,0:T(8,128)(2,1)} %weights_ref.3), custom_call_target="tpu_custom_call" | custom-call | tf_op jit(solution)/shard_map/prologue/pallas_call | solution.py:63
  4.0 82.1 %all_to_all.10 = bf16[128,32,128]{2,1,0:T(8,128)(2,1)} all-to-all(bf16[128,32,128]{2,1,0:T(8,128)(2,1)} %bitcast.16), channel_id=1, replica_groups=mesh['groups'=2,'row'=16,'col'=4,'ksplit'=2] {'row','col','ksplit'}, dimensions={0} | all-to-all | bytes 2097152 | tf_op jit(solution)/shard_map/all_to_all | solution.py:194
  86.1 2.8 %middle.1 = bf16[16,8,16,128]{3,2,1,0:T(8,128)(2,1)} custom-call(bf16[16,8,32,128]{3,2,1,0:T(8,128)(2,1)} %bitcast.15), custom_call_target="tpu_custom_call" | custom-call | tf_op jit(solution)/shard_map/middle/pallas_call | solution.py:167
  88.9 11.8 %all-to-all-start.1 = ((bf16[128,16,128]{2,1,0:T(8,128)(2,1)}), bf16[128,16,128]{2,1,0:T(8,128)(2,1)S(1)}, u32[]{:S(2)}, u32[]{:S(2)}) async-start(bf16[128,16,128]{2,1,0:T(8,128)(2,1)} %bitcast.17), calls=%async_computation.1 | async-start | bytes 1048576 | tf_op jit(solution)/shard_map/all_to_all | solution.py:196
  100.6 2.8 %output_gates.1 = f32[16,2,64,128]{3,2,1,0:T(8,128)} custom-call(bf16[2,16,64,128]{3,2,1,0:T(8,128)(2,1)} %bitcast.19, f32[1,128]{1,0:T(1,128)} %bitcast.22, f32[1,128]{1,0:T(1,128)} %bitcast.24, bf16[128,128]{1,0:T(8,128)(2,1)} %weights_ref.2), custom_call_target="tpu_custom_call" | custom-call | flops 67108864 | bytes 1572864 | tf_op jit(solution)/shard_map/output_gates/pallas_call | solution.py:104
  103.4 28.0 %all-to-all-done.1 = bf16[128,16,128]{2,1,0:T(8,128)(2,1)S(1)} async-done(((bf16[128,16,128]{2,1,0:T(8,128)(2,1)}), bf16[128,16,128]{2,1,0:T(8,128)(2,1)S(1)}, u32[]{:S(2)}, u32[]{:S(2)}) %all-to-all-start.1) | async-done | bytes 524320 | tf_op jit(solution)/shard_map/all_to_all | solution.py:196
  131.4 0.1 convert_reduce_fusion
  131.5 0.2 fusion.2
  131.7 0.0 copy-start.2
  131.7 0.0 copy-start.3
  131.7 0.6 copy-done.2
  132.4 0.0 copy-done.3
  132.4 0.3 fusion.5
  132.7 0.0 copy-done
  132.7 0.0 copy-start.1
  132.7 0.3 fusion.7
  133.1 0.9 copy-done.1
  134.0 0.2 fusion.6
  134.1 0.8 copy.14
  (2 shorter events, 0.0 us)
Async XLA Ops:
  0.0 132.7 %copy-start = (bf16[128,128]{1,0:T(8,128)(2,1)S(1)}, bf16[128,128]{1,0:T(8,128)(2,1)}, u32[]{:S(2)}) copy-start(bf16[128,128]{1,0:T(8,128)(2,1)} %param.17) | copy-start | bytes 98308
  88.9 42.5 %all-to-all-start.1 = ((bf16[128,16,128]{2,1,0:T(8,128)(2,1)}), bf16[128,16,128]{2,1,0:T(8,128)(2,1)S(1)}, u32[]{:S(2)}, u32[]{:S(2)}) async-start(bf16[128,16,128]{2,1,0:T(8,128)(2,1)} %bitcast.17), calls=%async_computation.1 | async-start | bytes 1048576 | tf_op jit(solution)/shard_map/all_to_all | solution.py:196
  131.7 0.7 copy-start.2
  131.7 0.7 copy-start.3
  132.7 1.2 copy-start.1

commit v4 on v3

--- a/solution.py
+++ b/solution.py
@@ -7,6 +7,7 @@
 
 F32 = jnp.float32
 BF16 = jnp.bfloat16
+GRANT = 24 << 20
 ACROSS = (((1,), (1,)), ((), ()))
 
 
@@ -85,48 +86,50 @@
     return both.reshape(hidden, rows, lanes)
 
 
-def gate_kernel(x_ref, gain_ref, shift_ref, weights_ref, gate_ref):
-    _, rows, cols, chans = x_ref.shape
+def gate_kernel(
+    x_ref, gain_ref, shift_ref, weights_ref, scale_ref, offset_ref, gate_ref, scaled_ref, moved_ref
+):
+    rows, cols, chans = x_ref.shape
     normed = norm_rows(x_ref[...].astype(F32), gain_ref[...], shift_ref[...])
     raised = jnp.dot(
-        normed.reshape(2 * rows * cols, chans), weights_ref[...], preferred_element_type=F32
-    )
-    gated = jax.nn.sigmoid(raised).reshape(2, rows, cols, chans)
-    gate_ref[:, 0] = gated[0]
-    gate_ref[:, 1] = gated[1]
-
-
-def output_gates(pair_state, input_gain, input_shift, output_gate):
+        normed.reshape(rows * cols, chans), weights_ref[...], preferred_element_type=F32
+    )
+    gate_ref[...] = jax.nn.sigmoid(raised).reshape(rows, cols, chans)
+    scaled_ref[...] = scale_ref[...]
+    moved_ref[...] = offset_ref[...]
+
+
+def output_gates(pair_state, input_gain, input_shift, output_gate, final_gain, final_shift):
     rows, cols, chans = pair_state.shape
-    half = rows // 2
-    step = 8
-    still = lambda s: (0, 0)
+    hidden = final_gain.shape[0]
+    vmem = pl.BlockSpec(memory_space=pltpu.VMEM)
     return pl.pallas_call(
         gate_kernel,
-        grid=(half // step,),
-        out_shape=jax.ShapeDtypeStruct((half, 2, cols, chans), F32),
-        in_specs=[
-            pl.BlockSpec((2, step, cols, chans), lambda s: (0, s, 0, 0)),
-            pl.BlockSpec((1, chans), still),
-            pl.BlockSpec((1, chans), still),
-            pl.BlockSpec((chans, chans), still),
-        ],
-        out_specs=pl.BlockSpec((step, 2, cols, chans), lambda s: (s, 0, 0, 0)),
+        out_shape=(
+            jax.ShapeDtypeStruct((rows, cols, chans), F32),
+            jax.ShapeDtypeStruct((1, hidden), F32),
+            jax.ShapeDtypeStruct((1, hidden), F32),
+        ),
+        in_specs=[vmem] * 6,
+        out_specs=(vmem,) * 3,
         cost_estimate=pl.CostEstimate(
             flops=2 * rows * cols * chans * chans,
             bytes_accessed=6 * rows * cols * chans,
             transcendentals=rows * cols * chans,
         ),
+        compiler_params=pltpu.CompilerParams(vmem_limit_bytes=GRANT),
         name="output_gates",
     )(
-        pair_state.reshape(2, half, cols, chans),
+        pair_state,
         input_gain.reshape(1, -1),
         input_shift.reshape(1, -1),
         output_gate,
-    )
-
-
-def middle_kernel(in_ref, out_ref):
+        final_gain.reshape(1, -1),
+        final_shift.reshape(1, -1),
+    )
+
+
+def middle_kernel(in_ref, out_ref, product_ref):
     nrow, ncol, rows, lanes = in_ref.shape
     half = rows // 2
     cols = lanes // 2
@@ -154,11 +157,11 @@
         preferred_element_type=F32,
     )
     for k in range(0, ncol, 2):
-        tile = product[:, k * cols : (k + 2) * cols].reshape(nrow, rows, lanes)
-        top = tile[:, :half]
-        bottom = tile[:, half:]
-        out_ref[:, k] = jnp.where(low, top, pltpu.roll(bottom, cols, 2)).astype(BF16)
-        out_ref[:, k + 1] = jnp.where(low, pltpu.roll(top, cols, 2), bottom).astype(BF16)
+        product_ref[k // 2] = product[:, k * cols : (k + 2) * cols]
+        even = product_ref[k // 2, pl.ds(0, nrow * half, 2), :].reshape(nrow, half, lanes)
+        uneven = product_ref[k // 2, pl.ds(1, nrow * half, 2), :].reshape(nrow, half, lanes)
+        out_ref[:, k] = jnp.where(low, even, pltpu.roll(uneven, cols, 2)).astype(BF16)
+        out_ref[:, k + 1] = jnp.where(low, pltpu.roll(even, cols, 2), uneven).astype(BF16)
 
 
 def middle(parts, row_count, col_count):
@@ -169,6 +172,8 @@
         out_shape=jax.ShapeDtypeStruct((row_count, col_count, rows // 2, lanes), BF16),
         in_specs=[vmem],
         out_specs=vmem,
+        scratch_shapes=[pltpu.VMEM((col_count // 2, row_count * rows, lanes), F32)],
+        compiler_params=pltpu.CompilerParams(vmem_limit_bytes=GRANT),
         name="middle",
     )(parts.reshape(row_count, col_count, rows, lanes))
     return returned.reshape(count, rows // 2, lanes)
@@ -190,7 +195,9 @@
     row_count = lax.axis_size("row")
     col_count = lax.axis_size(("col", "ksplit"))
     both = prologue(pair_state, residue_mask, input_gain, input_shift, left_right)
-    gates = output_gates(pair_state, input_gain, input_shift, output_gate)
+    gates, scale, offset = output_gates(
+        pair_state, input_gain, input_shift, output_gate, final_gain, final_shift
+    )
     parts = lax.all_to_all(both, every, split_axis=0, concat_axis=0, tiled=True)
     returned = middle(parts, row_count, col_count)
     received = lax.all_to_all(returned, every, split_axis=0, concat_axis=0, tiled=True)
@@ -199,15 +206,12 @@
     centred = mixed - average
     spread = jnp.mean(centred * centred, axis=0, keepdims=True)
     normed_out = (
-        centred * lax.rsqrt(spread + 1e-05) * final_gain[:, None, None]
-        + final_shift[:, None, None]
+        centred * lax.rsqrt(spread + 1e-05) * scale.reshape(-1, 1, 1) + offset.reshape(-1, 1, 1)
     ).astype(BF16)
     projected_out = jnp.einsum(
         "hrl,hc->rlc", normed_out, output_weight, preferred_element_type=F32
     )
-    update = gates * projected_out.reshape(tile_rows // 2, 2, tile_cols, channels)
-    update = update.transpose(1, 0, 2, 3).astype(BF16)
-    return update.reshape(tile_rows, tile_cols, channels)
+    return (gates * projected_out.reshape(tile_rows, tile_cols, channels)).astype(BF16)
 
 
 def solution(mesh):

time: 135 us -> 133 us (0.985)
  Pallas kernels: 9.56 us -> 6.42 us
  local copies, waits for them, and re-layouts: 2.36 us -> 0.65 us
    pallas_call x1, Pallas kernels: 2.77 us -> 0.78 us  [output_gates(): pl.pallas_call(gate_kernel, out_shape=(jax.ShapeDtypeStruct((rows, cols,...]
  transfers between devices with their start and end apart: 1 -> 1, of which waited for: 1 -> 1; matrix products, arithmetic and copies ran while one was open for 0% -> 0% of each run, Pallas kernels for 2% -> 1%
where the time goes in v4:
time: 133 us; the launch traced here: 132 us
  blocking collectives  82 us (62%)
  waiting for transfers between devices  29.3 us (22%)
  starting transfers between devices  11.9 us (9%)
  Pallas kernels  6.42 us (5%)
  other arithmetic  1.65 us (1%)
    all_to_all x1, blocking collectives, body(): parts = lax.all_to_all(both, every, split_axis=0, concat_axis=0, tiled=True)  82 us
    all_to_all x1, waiting for transfers between devices, body(): lax.all_to_all(returned, every, split_axis=0, concat_axis=0, tiled=True)  29.3 us
    all_to_all x1, starting transfers between devices, body(): lax.all_to_all(returned, every, split_axis=0, concat_axis=0, tiled=True)  11.9 us
    pallas_call x1, Pallas kernels, prologue(): pl.pallas_call(prologue_kernel, grid=(half // step,), out_shape=jax.Shape...  4.03 us
  transfers between devices with their start and end apart: 1, of which 1 were waited for; matrix products, arithmetic and copies ran while one was open for 0% of the time, Pallas kernels for 1%

profile of v4, /device:TPU:33, one launch (start us, length us, event | category | flops | bytes accessed | tf_op | source)
XLA Modules:
  0.0 132.3 jit_solution(16843085305141656559)
XLA Ops:
  0.0 0.0 copy-start
  0.0 4.0 %prologue.1 = bf16[128,2,16,128]{3,2,1,0:T(8,128)(2,1)} custom-call(s32[512]{0:T(512)} %live_ref.1, s32[4,128]{1,0:T(4,128)} %bitcast.27, bf16[2,16,64,128]{3,2,1,0:T(8,128)(2,1)} %bitcast.16, f32[1,128]{1,0:T(1,128)} %bitcast.17, f32[1,128]{1,0:T(1,128)} %bitcast.19, bf16[128,512]{1,0:T(8,128)(2,1)} %weights_ref.3), custom_call_target="tpu_custom_call" | custom-call | tf_op jit(solution)/shard_map/prologue/pallas_call | solution.py:64
  4.0 82.0 %all_to_all.10 = bf16[128,32,128]{2,1,0:T(8,128)(2,1)S(1)} all-to-all(bf16[128,32,128]{2,1,0:T(8,128)(2,1)} %bitcast.26), channel_id=1, replica_groups=mesh['groups'=2,'row'=16,'col'=4,'ksplit'=2] {'row','col','ksplit'}, dimensions={0} | all-to-all | bytes 2097152 | tf_op jit(solution)/shard_map/all_to_all | solution.py:201
  86.0 1.6 %middle.1 = bf16[16,8,16,128]{3,2,1,0:T(8,128)(2,1)} custom-call(bf16[16,8,32,128]{3,2,1,0:T(8,128)(2,1)S(1)} %bitcast.15), custom_call_target="tpu_custom_call" | custom-call | tf_op jit(solution)/shard_map/middle/pallas_call | solution.py:170
  87.6 0.0 copy-start.1
  87.6 0.0 copy-start.2
  87.6 0.0 copy-start.6
  87.6 11.9 %all-to-all-start.1 = ((bf16[128,16,128]{2,1,0:T(8,128)(2,1)}), bf16[128,16,128]{2,1,0:T(8,128)(2,1)S(1)}, u32[]{:S(2)}, u32[]{:S(2)}) async-start(bf16[128,16,128]{2,1,0:T(8,128)(2,1)} %bitcast.8), calls=%async_computation.1 | async-start | bytes 1048576 | tf_op jit(solution)/shard_map/all_to_all | solution.py:203
  99.5 0.0 copy-start.3
  99.5 0.0 copy-start.4
  99.5 0.0 copy-start.5
  99.6 0.0 copy-done.1
  99.6 0.0 copy-done.2
  99.6 0.0 copy-done.6
  99.6 0.6 copy-done.3
  100.2 0.0 copy-done.4
  100.2 0.0 copy-done.5
  100.2 0.8 output_gates.1
  101.0 29.3 %all-to-all-done.1 = bf16[128,16,128]{2,1,0:T(8,128)(2,1)S(1)} async-done(((bf16[128,16,128]{2,1,0:T(8,128)(2,1)}), bf16[128,16,128]{2,1,0:T(8,128)(2,1)S(1)}, u32[]{:S(2)}, u32[]{:S(2)}) %all-to-all-start.1) | async-done | bytes 524320 | tf_op jit(solution)/shard_map/all_to_all | solution.py:203
  130.3 0.1 convert_reduce_fusion
  130.4 0.2 fusion.2
  130.6 0.3 fusion.5
  131.0 0.0 copy-done
  131.0 0.3 fusion.6
  131.3 1.0 multiply_convert_fusion
  (2 shorter events, 0.0 us)
Async XLA Ops:
  0.0 131.0 %copy-start = (bf16[128,128]{1,0:T(8,128)(2,1)S(1)}, bf16[128,128]{1,0:T(8,128)(2,1)}, u32[]{:S(2)}) copy-start(bf16[128,128]{1,0:T(8,128)(2,1)} %param.17) | copy-start | bytes 98308
  87.6 11.9 %copy-start.1 = (bf16[32,64,128]{2,1,0:T(8,128)(2,1)S(1)}, bf16[32,64,128]{2,1,0:T(8,128)(2,1)}, u32[]{:S(2)}) copy-start(bf16[32,64,128]{2,1,0:T(8,128)(2,1)} %x_ref.1) | copy-start | bytes 1572868
  87.6 11.9 %copy-start.2 = (bf16[128,128]{1,0:T(8,128)(2,1)S(1)}, bf16[128,128]{1,0:T(8,128)(2,1)}, u32[]{:S(2)}) copy-start(bf16[128,128]{1,0:T(8,128)(2,1)} %weights_ref.2) | copy-start | bytes 98308
  87.6 12.0 %copy-start.6 = (f32[128]{0:T(128)S(1)}, f32[128]{0:T(128)}, u32[]{:S(2)}) copy-start(f32[128]{0:T(128)} %param.16) | copy-start | bytes 1540
  87.6 42.6 %all-to-all-start.1 = ((bf16[128,16,128]{2,1,0:T(8,128)(2,1)}), bf16[128,16,128]{2,1,0:T(8,128)(2,1)S(1)}, u32[]{:S(2)}, u32[]{:S(2)}) async-start(bf16[128,16,128]{2,1,0:T(8,128)(2,1)} %bitcast.8), calls=%async_computation.1 | async-start | bytes 1048576 | tf_op jit(solution)/shard_map/all_to_all | solution.py:203
  99.5 0.7 copy-start.3
  99.5 0.7 copy-start.4
  99.5 0.7 copy-start.5

commit v5 on v4

--- a/solution.py
+++ b/solution.py
@@ -129,11 +129,12 @@
     )
 
 
-def middle_kernel(in_ref, out_ref, product_ref):
+def middle_kernel(in_ref, scale_ref, out_ref, passed_ref, product_ref):
     nrow, ncol, rows, lanes = in_ref.shape
     half = rows // 2
     cols = lanes // 2
     low = lax.broadcasted_iota(jnp.int32, (1, 1, lanes), 2) < cols
+    passed_ref[...] = scale_ref[...]
 
     def sides(k):
         top = in_ref[:, k, :half].astype(F32)
@@ -164,19 +165,22 @@
         out_ref[:, k + 1] = jnp.where(low, pltpu.roll(even, cols, 2), uneven).astype(BF16)
 
 
-def middle(parts, row_count, col_count):
+def middle(parts, scale, row_count, col_count):
     count, rows, lanes = parts.shape
     vmem = pl.BlockSpec(memory_space=pltpu.VMEM)
-    returned = pl.pallas_call(
+    returned, passed = pl.pallas_call(
         middle_kernel,
-        out_shape=jax.ShapeDtypeStruct((row_count, col_count, rows // 2, lanes), BF16),
-        in_specs=[vmem],
-        out_specs=vmem,
+        out_shape=(
+            jax.ShapeDtypeStruct((row_count, col_count, rows // 2, lanes), BF16),
+            jax.ShapeDtypeStruct(scale.shape, F32),
+        ),
+        in_specs=[vmem] * 2,
+        out_specs=(vmem,) * 2,
         scratch_shapes=[pltpu.VMEM((col_count // 2, row_count * rows, lanes), F32)],
         compiler_params=pltpu.CompilerParams(vmem_limit_bytes=GRANT),
         name="middle",
-    )(parts.reshape(row_count, col_count, rows, lanes))
-    return returned.reshape(count, rows // 2, lanes)
+    )(parts.reshape(row_count, col_count, rows, lanes), scale)
+    return returned.reshape(count, rows // 2, lanes), passed
 
 
 def body(
@@ -199,7 +203,7 @@
         pair_state, input_gain, input_shift, output_gate, final_gain, final_shift
     )
     parts = lax.all_to_all(both, every, split_axis=0, concat_axis=0, tiled=True)
-    returned = middle(parts, row_count, col_count)
+    returned, scale = middle(parts, scale, row_count, col_count)
     received = lax.all_to_all(returned, every, split_axis=0, concat_axis=0, tiled=True)
     mixed = received.astype(F32)
     average = jnp.mean(mixed, axis=0, keepdims=True)

time: 133 us -> 132 us (level)
  blocking collectives: 82 us -> 42.3 us
  waiting for transfers between devices: 29.3 us -> 49.5 us
  starting transfers between devices: 11.9 us -> 31.1 us
    all_to_all x1, blocking collectives: 82 us -> 42.3 us  [body(): lax.all_to_all(returned, every, split_axis=0, concat_axis=0, tiled=True)]
    all_to_all x1, waiting for transfers between devices: 29.3 us -> 49.5 us  [body(): parts = lax.all_to_all(both, every, split_axis=0, concat_axis=0, tiled=True)]
    all_to_all x1, starting transfers between devices: 11.9 us -> 31.1 us  [body(): parts = lax.all_to_all(both, every, split_axis=0, concat_axis=0, tiled=True)]
where the time goes in v5:
time: 132 us; the launch traced here: 131 us
  waiting for transfers between devices  49.5 us (38%)
  blocking collectives  42.3 us (32%)
  starting transfers between devices  31.1 us (24%)
  Pallas kernels  5.64 us (4%)
  other arithmetic  1.65 us (1%)
    all_to_all x1, waiting for transfers between devices, body(): parts = lax.all_to_all(both, every, split_axis=0, concat_axis=0, tiled=True)  49.5 us
    all_to_all x1, blocking collectives, body(): lax.all_to_all(returned, every, split_axis=0, concat_axis=0, tiled=True)  42.3 us
    all_to_all x1, starting transfers between devices, body(): parts = lax.all_to_all(both, every, split_axis=0, concat_axis=0, tiled=True)  31.1 us
    pallas_call x1, Pallas kernels, prologue(): pl.pallas_call(prologue_kernel, grid=(half // step,), out_shape=jax.Shape...  4.03 us
  transfers between devices with their start and end apart: 1, of which 1 were waited for; matrix products, arithmetic and copies ran while one was open for 0% of the time, Pallas kernels for 1%

profile of v5, /device:TPU:33, one launch (start us, length us, event | category | flops | bytes accessed | tf_op | source)
XLA Modules:
  0.0 131.3 jit_solution(151964760657060626)
XLA Ops:
  0.0 0.0 copy-start
  0.0 4.0 %prologue.1 = bf16[128,2,16,128]{3,2,1,0:T(8,128)(2,1)} custom-call(s32[512]{0:T(512)} %live_ref.1, s32[4,128]{1,0:T(4,128)} %bitcast.28, bf16[2,16,64,128]{3,2,1,0:T(8,128)(2,1)} %bitcast.16, f32[1,128]{1,0:T(1,128)} %bitcast.18, f32[1,128]{1,0:T(1,128)} %bitcast.20, bf16[128,512]{1,0:T(8,128)(2,1)} %weights_ref.3), custom_call_target="tpu_custom_call" | custom-call | tf_op jit(solution)/shard_map/prologue/pallas_call | solution.py:64
  4.0 0.0 copy-start.1
  4.0 0.0 copy-start.2
  4.0 0.0 copy-start.6
  4.0 31.1 %all-to-all-start = ((bf16[128,32,128]{2,1,0:T(8,128)(2,1)}), bf16[128,32,128]{2,1,0:T(8,128)(2,1)S(1)}, u32[]{:S(2)}, u32[]{:S(2)}) async-start(bf16[128,32,128]{2,1,0:T(8,128)(2,1)} %bitcast.26), calls=%async_computation | async-start | bytes 2097152 | tf_op jit(solution)/shard_map/all_to_all | solution.py:205
  35.2 0.0 copy-start.3
  35.2 0.0 copy-start.4
  35.2 0.0 copy-start.5
  35.2 0.0 copy-done.1
  35.2 0.0 copy-done.2
  35.3 0.0 copy-done.6
  35.3 0.6 copy-done.3
  35.9 0.0 copy-done.4
  35.9 0.0 copy-done.5
  35.9 0.8 output_gates.1
  36.7 49.5 %all-to-all-done = bf16[128,32,128]{2,1,0:T(8,128)(2,1)S(1)} async-done(((bf16[128,32,128]{2,1,0:T(8,128)(2,1)}), bf16[128,32,128]{2,1,0:T(8,128)(2,1)S(1)}, u32[]{:S(2)}, u32[]{:S(2)}) %all-to-all-start) | async-done | bytes 1048608 | tf_op jit(solution)/shard_map/all_to_all | solution.py:205
  86.2 0.8 middle.1
  87.0 42.3 %all_to_all.10 = bf16[128,16,128]{2,1,0:T(8,128)(2,1)S(1)} all-to-all(bf16[128,16,128]{2,1,0:T(8,128)(2,1)S(1)} %bitcast.17), channel_id=1, replica_groups=mesh['groups'=2,'row'=16,'col'=4,'ksplit'=2] {'row','col','ksplit'}, dimensions={0} | all-to-all | bytes 1048576 | tf_op jit(solution)/shard_map/all_to_all | solution.py:207
  129.3 0.1 convert_reduce_fusion
  129.5 0.2 fusion.2
  129.7 0.3 fusion.5
  130.0 0.0 copy-done
  130.0 0.3 fusion.6
  130.4 1.0 multiply_convert_fusion
  (2 shorter events, 0.0 us)
Async XLA Ops:
  0.0 130.0 %copy-start = (bf16[128,128]{1,0:T(8,128)(2,1)S(1)}, bf16[128,128]{1,0:T(8,128)(2,1)}, u32[]{:S(2)}) copy-start(bf16[128,128]{1,0:T(8,128)(2,1)} %param.17) | copy-start | bytes 98308
  4.0 31.2 %copy-start.1 = (bf16[32,64,128]{2,1,0:T(8,128)(2,1)S(1)}, bf16[32,64,128]{2,1,0:T(8,128)(2,1)}, u32[]{:S(2)}) copy-start(bf16[32,64,128]{2,1,0:T(8,128)(2,1)} %x_ref.1) | copy-start | bytes 1572868
  4.0 31.2 %copy-start.2 = (bf16[128,128]{1,0:T(8,128)(2,1)S(1)}, bf16[128,128]{1,0:T(8,128)(2,1)}, u32[]{:S(2)}) copy-start(bf16[128,128]{1,0:T(8,128)(2,1)} %weights_ref.2) | copy-start | bytes 98308
  4.0 31.2 %copy-start.6 = (f32[128]{0:T(128)S(1)}, f32[128]{0:T(128)}, u32[]{:S(2)}) copy-start(f32[128]{0:T(128)} %param.16) | copy-start | bytes 1540
  4.0 82.1 %all-to-all-start = ((bf16[128,32,128]{2,1,0:T(8,128)(2,1)}), bf16[128,32,128]{2,1,0:T(8,128)(2,1)S(1)}, u32[]{:S(2)}, u32[]{:S(2)}) async-start(bf16[128,32,128]{2,1,0:T(8,128)(2,1)} %bitcast.26), calls=%async_computation | async-start | bytes 2097152 | tf_op jit(solution)/shard_map/all_to_all | solution.py:205
  35.2 0.7 copy-start.3
  35.2 0.7 copy-start.4
  35.2 0.7 copy-start.5

commit v6 on v5

--- a/solution.py
+++ b/solution.py
@@ -94,7 +94,7 @@
     raised = jnp.dot(
         normed.reshape(rows * cols, chans), weights_ref[...], preferred_element_type=F32
     )
-    gate_ref[...] = jax.nn.sigmoid(raised).reshape(rows, cols, chans)
+    gate_ref[...] = jax.nn.sigmoid(raised).reshape(gate_ref.shape)
     scaled_ref[...] = scale_ref[...]
     moved_ref[...] = offset_ref[...]
 
@@ -106,7 +106,7 @@
     return pl.pallas_call(
         gate_kernel,
         out_shape=(
-            jax.ShapeDtypeStruct((rows, cols, chans), F32),
+            jax.ShapeDtypeStruct((rows // 2, 2 * cols, chans), F32),
             jax.ShapeDtypeStruct((1, hidden), F32),
             jax.ShapeDtypeStruct((1, hidden), F32),
         ),
@@ -215,7 +215,8 @@
     projected_out = jnp.einsum(
         "hrl,hc->rlc", normed_out, output_weight, preferred_element_type=F32
     )
-    return (gates * projected_out.reshape(tile_rows, tile_cols, channels)).astype(BF16)
+    update = (gates.reshape(projected_out.shape) * projected_out).astype(BF16)
+    return update.reshape(tile_rows, tile_cols, channels)
 
 
 def solution(mesh):

time: 132 us -> 131 us (level)
  no operation moved by 1% of the time
where the time goes in v6:
time: 131 us
  waiting for transfers between devices  49.5 us (38%)
  blocking collectives  42.3 us (32%)
  starting transfers between devices  31.1 us (24%)
  Pallas kernels  5.64 us (4%)
    all_to_all x1, waiting for transfers between devices, body(): parts = lax.all_to_all(both, every, split_axis=0, concat_axis=0, tiled=True)  49.5 us
    all_to_all x1, blocking collectives, body(): lax.all_to_all(returned, every, split_axis=0, concat_axis=0, tiled=True)  42.3 us
    all_to_all x1, starting transfers between devices, body(): parts = lax.all_to_all(both, every, split_axis=0, concat_axis=0, tiled=True)  31.1 us
    pallas_call x1, Pallas kernels, prologue(): pl.pallas_call(prologue_kernel, grid=(half // step,), out_shape=jax.Shape...  4.03 us
  transfers between devices with their start and end apart: 1, of which 1 were waited for; matrix products, arithmetic and copies ran while one was open for 0% of the time, Pallas kernels for 1%

profile of v6, /device:TPU:33, one launch (start us, length us, event | category | flops | bytes accessed | tf_op | source)
XLA Modules:
  0.0 131.1 jit_solution(706950389902871597)
XLA Ops:
  0.0 0.0 copy-start
  0.0 4.0 %prologue.1 = bf16[128,2,16,128]{3,2,1,0:T(8,128)(2,1)} custom-call(s32[512]{0:T(512)} %live_ref.1, s32[4,128]{1,0:T(4,128)} %bitcast.27, bf16[2,16,64,128]{3,2,1,0:T(8,128)(2,1)} %bitcast.16, f32[1,128]{1,0:T(1,128)} %bitcast.18, f32[1,128]{1,0:T(1,128)} %bitcast.20, bf16[128,512]{1,0:T(8,128)(2,1)} %weights_ref.3), custom_call_target="tpu_custom_call" | custom-call | tf_op jit(solution)/shard_map/prologue/pallas_call | solution.py:64
  4.0 0.0 copy-start.1
  4.0 0.0 copy-start.2
  4.0 0.0 copy-start.6
  4.0 31.1 %all-to-all-start = ((bf16[128,32,128]{2,1,0:T(8,128)(2,1)}), bf16[128,32,128]{2,1,0:T(8,128)(2,1)S(1)}, u32[]{:S(2)}, u32[]{:S(2)}) async-start(bf16[128,32,128]{2,1,0:T(8,128)(2,1)} %bitcast.26), calls=%async_computation | async-start | bytes 2097152 | tf_op jit(solution)/shard_map/all_to_all | solution.py:205
  35.2 0.0 copy-start.3
  35.2 0.0 copy-start.4
  35.2 0.0 copy-start.5
  35.2 0.0 copy-done.1
  35.2 0.0 copy-done.2
  35.3 0.0 copy-done.6
  35.3 0.6 copy-done.3
  35.9 0.0 copy-done.4
  35.9 0.0 copy-done.5
  35.9 0.8 output_gates.1
  36.7 49.5 %all-to-all-done = bf16[128,32,128]{2,1,0:T(8,128)(2,1)S(1)} async-done(((bf16[128,32,128]{2,1,0:T(8,128)(2,1)}), bf16[128,32,128]{2,1,0:T(8,128)(2,1)S(1)}, u32[]{:S(2)}, u32[]{:S(2)}) %all-to-all-start) | async-done | bytes 1048608 | tf_op jit(solution)/shard_map/all_to_all | solution.py:205
  86.2 0.8 middle.1
  87.0 42.3 %all_to_all.10 = bf16[128,16,128]{2,1,0:T(8,128)(2,1)S(1)} all-to-all(bf16[128,16,128]{2,1,0:T(8,128)(2,1)S(1)} %bitcast.17), channel_id=1, replica_groups=mesh['groups'=2,'row'=16,'col'=4,'ksplit'=2] {'row','col','ksplit'}, dimensions={0} | all-to-all | bytes 1048576 | tf_op jit(solution)/shard_map/all_to_all | solution.py:207
  129.3 0.1 convert_reduce_fusion
  129.5 0.2 fusion.3
  129.7 0.3 fusion.6
  130.0 0.0 copy-done
  130.0 1.1 fusion
  (2 shorter events, 0.0 us)
Async XLA Ops:
  0.0 130.0 %copy-start = (bf16[128,128]{1,0:T(8,128)(2,1)S(1)}, bf16[128,128]{1,0:T(8,128)(2,1)}, u32[]{:S(2)}) copy-start(bf16[128,128]{1,0:T(8,128)(2,1)} %param.17) | copy-start | bytes 98308
  4.0 31.2 %copy-start.1 = (bf16[32,64,128]{2,1,0:T(8,128)(2,1)S(1)}, bf16[32,64,128]{2,1,0:T(8,128)(2,1)}, u32[]{:S(2)}) copy-start(bf16[32,64,128]{2,1,0:T(8,128)(2,1)} %x_ref.1) | copy-start | bytes 1572868
  4.0 31.2 %copy-start.2 = (bf16[128,128]{1,0:T(8,128)(2,1)S(1)}, bf16[128,128]{1,0:T(8,128)(2,1)}, u32[]{:S(2)}) copy-start(bf16[128,128]{1,0:T(8,128)(2,1)} %weights_ref.2) | copy-start | bytes 98308
  4.0 31.2 %copy-start.6 = (f32[128]{0:T(128)S(1)}, f32[128]{0:T(128)}, u32[]{:S(2)}) copy-start(f32[128]{0:T(128)} %param.16) | copy-start | bytes 1540
  4.0 82.1 %all-to-all-start = ((bf16[128,32,128]{2,1,0:T(8,128)(2,1)}), bf16[128,32,128]{2,1,0:T(8,128)(2,1)S(1)}, u32[]{:S(2)}, u32[]{:S(2)}) async-start(bf16[128,32,128]{2,1,0:T(8,128)(2,1)} %bitcast.26), calls=%async_computation | async-start | bytes 2097152 | tf_op jit(solution)/shard_map/all_to_all | solution.py:205
  35.2 0.7 copy-start.3
  35.2 0.7 copy-start.4
  35.2 0.7 copy-start.5

commit v7 on v6

--- a/solution.py
+++ b/solution.py
@@ -18,72 +18,93 @@
     return (centred * lax.rsqrt(spread + 1e-05) * norm_gain + norm_shift).astype(BF16)
 
 
-def prologue_kernel(live_ref, cols_ref, x_ref, gain_ref, shift_ref, weights_ref, both_ref):
-    _, step, cols, chans = x_ref.shape
+def prologue_kernel(
+    live_ref, cols_ref, x_ref, gain_ref, shift_ref, weights_ref, both_ref, turned_ref, normed_ref
+):
+    rows, cols, chans = x_ref.shape
     hidden = weights_ref.shape[1] // 4
+    block = both_ref.shape[0]
     lanes = 2 * cols
-    half = step * pl.num_programs(0)
-    row_start = lax.axis_index("row") * (2 * half) + pl.program_id(0) * step
+    half = rows // 2
+    step = 8
+    nth = pl.program_id(0)
+
+    @pl.when(nth == 0)
+    def _():
+        turned_ref[...] = weights_ref[...].T
+        for start in range(0, rows, step):
+            data = x_ref[start : start + step].astype(F32)
+            normed_ref[start : start + step] = norm_rows(data, gain_ref[...], shift_ref[...])
+
+    row_start = lax.axis_index("row") * rows
     col_index = lax.axis_index("col") * lax.axis_size("ksplit") + lax.axis_index("ksplit")
     low = lax.broadcasted_iota(jnp.int32, (1, lanes), 1) < cols
     pair = cols_ref[pl.ds(col_index // 2, 1), :].astype(F32)
     swapped = pltpu.roll(pair, cols, 1)
-    own_low = jnp.where(low, pair, swapped)
-    own_high = jnp.where(low, swapped, pair)
     odd = (col_index % 2).astype(F32)
-    col_live = own_high * odd + own_low * (1.0 - odd)
-    top = norm_rows(x_ref[0].astype(F32), gain_ref[...], shift_ref[...])
-    bottom = norm_rows(x_ref[1].astype(F32), gain_ref[...], shift_ref[...])
-    straight = jnp.stack([top, bottom], axis=1).reshape(step * lanes, chans)
-    crossed = jnp.stack([bottom, top], axis=1).reshape(step * lanes, chans)
-    turned = weights_ref[...].T
-    left = lax.dot_general(turned[: 2 * hidden], straight, ACROSS, preferred_element_type=F32)
-    right = lax.dot_general(turned[2 * hidden :], crossed, ACROSS, preferred_element_type=F32)
-    left = left[:hidden] * jax.nn.sigmoid(left[hidden:])
-    right = right[:hidden] * jax.nn.sigmoid(right[hidden:])
-    upper, lower = [], []
-    for t in range(step):
-        live_top = live_ref[row_start + t].astype(F32)
-        live_bottom = live_ref[row_start + half + t].astype(F32)
-        span = slice(t * lanes, (t + 1) * lanes)
-        from_left = left[:, span] * (jnp.where(low, live_top, live_bottom) * col_live)
-        from_right = right[:, span] * (jnp.where(low, live_bottom, live_top) * col_live)
-        upper.append(jnp.where(low, from_left, from_right))
-        lower.append(jnp.where(low, from_right, from_left))
-    both_ref[:, 0] = jnp.swapaxes(jnp.stack(upper, axis=0), 0, 1).astype(BF16)
-    both_ref[:, 1] = jnp.swapaxes(jnp.stack(lower, axis=0), 0, 1).astype(BF16)
+    col_live = jnp.where(low, swapped, pair) * odd + jnp.where(low, pair, swapped) * (1.0 - odd)
+    own = [
+        turned_ref[pl.ds(pl.multiple_of(part * hidden + nth * block, block), block), :]
+        for part in range(4)
+    ]
+    left_weights = jnp.concatenate(own[:2], axis=0)
+    right_weights = jnp.concatenate(own[2:], axis=0)
+    for base in range(0, half, step):
+        top = normed_ref[base : base + step]
+        bottom = normed_ref[half + base : half + base + step]
+        straight = jnp.stack([top, bottom], axis=1).reshape(step * lanes, chans)
+        crossed = jnp.stack([bottom, top], axis=1).reshape(step * lanes, chans)
+        left = lax.dot_general(left_weights, straight, ACROSS, preferred_element_type=F32)
+        right = lax.dot_general(right_weights, crossed, ACROSS, preferred_element_type=F32)
+        left = left[:block] * jax.nn.sigmoid(left[block:])
+        right = right[:block] * jax.nn.sigmoid(right[block:])
+        upper, lower = [], []
+        for t in range(step):
+            live_top = live_ref[row_start + base + t].astype(F32)
+            live_bottom = live_ref[row_start + half + base + t].astype(F32)
+            span = slice(t * lanes, (t + 1) * lanes)
+            from_left = left[:, span] * (jnp.where(low, live_top, live_bottom) * col_live)
+            from_right = right[:, span] * (jnp.where(low, live_bottom, live_top) * col_live)
+            upper.append(jnp.where(low, from_left, from_right))
+            lower.append(jnp.where(low, from_right, from_left))
+        both_ref[:, base : base + step] = jnp.swapaxes(jnp.stack(upper), 0, 1).astype(BF16)
+        both_ref[:, half + base : half + base + step] = jnp.swapaxes(
+            jnp.stack(lower), 0, 1
+        ).astype(BF16)
 
 
 def prologue(pair_state, residue_mask, input_gain, input_shift, left_right):
     rows, cols, chans = pair_state.shape
     hidden = left_right.shape[1] // 4
-    half = rows // 2
-    step = 8
     lanes = 2 * cols
+    block = hidden // 2
     still = lambda s: (0, 0)
-    both = pl.pallas_call(
+    return pl.pallas_call(
         prologue_kernel,
-        grid=(half // step,),
-        out_shape=jax.ShapeDtypeStruct((hidden, 2, half, lanes), BF16),
+        grid=(hidden // block,),
+        out_shape=jax.ShapeDtypeStruct((hidden, rows, lanes), BF16),
         in_specs=[
             pl.BlockSpec(memory_space=pltpu.SMEM),
             pl.BlockSpec((residue_mask.shape[0] // lanes, lanes), still),
-            pl.BlockSpec((2, step, cols, chans), lambda s: (0, s, 0, 0)),
+            pl.BlockSpec((rows, cols, chans), lambda s: (0, 0, 0)),
             pl.BlockSpec((1, chans), still),
             pl.BlockSpec((1, chans), still),
             pl.BlockSpec((chans, 4 * hidden), still),
         ],
-        out_specs=pl.BlockSpec((hidden, 2, step, lanes), lambda s: (0, 0, s, 0)),
+        out_specs=pl.BlockSpec((block, rows, lanes), lambda s: (s, 0, 0)),
+        scratch_shapes=[
+            pltpu.VMEM((4 * hidden, chans), BF16),
+            pltpu.VMEM((rows, cols, chans), BF16),
+        ],
         name="prologue",
     )(
         residue_mask,
         residue_mask.reshape(-1, lanes),
-        pair_state.reshape(2, half, cols, chans),
+        pair_state,
         input_gain.reshape(1, -1),
         input_shift.reshape(1, -1),
         left_right,
     )
-    return both.reshape(hidden, rows, lanes)
 
 
 def gate_kernel(

time: 131 us -> 131 us (level)
  no operation moved by 1% of the time
where the time goes in v7:
time: 131 us
  waiting for transfers between devices  49.5 us (38%)
  blocking collectives  42.3 us (32%)
  starting transfers between devices  31.1 us (24%)
  Pallas kernels  5.59 us (4%)
    all_to_all x1, waiting for transfers between devices, body(): parts = lax.all_to_all(both, every, split_axis=0, concat_axis=0, tiled=True)  49.5 us
    all_to_all x1, blocking collectives, body(): lax.all_to_all(returned, every, split_axis=0, concat_axis=0, tiled=True)  42.3 us
    all_to_all x1, starting transfers between devices, body(): parts = lax.all_to_all(both, every, split_axis=0, concat_axis=0, tiled=True)  31.1 us
    pallas_call x1, Pallas kernels, prologue(): pl.pallas_call(prologue_kernel, grid=(hidden // block,), out_shape=jax.Sh...  3.98 us
  transfers between devices with their start and end apart: 1, of which 1 were waited for; matrix products, arithmetic and copies ran while one was open for 0% of the time, Pallas kernels for 1%

profile of v7, /device:TPU:33, one launch (start us, length us, event | category | flops | bytes accessed | tf_op | source)
XLA Modules:
  0.0 131.1 jit_solution(6750547360475174332)
XLA Ops:
  0.0 0.0 copy-start
  0.0 4.0 %prologue.1 = bf16[128,32,128]{2,1,0:T(8,128)(2,1)} custom-call(s32[512]{0:T(512)} %live_ref.1, s32[4,128]{1,0:T(4,128)} %bitcast.23, bf16[32,64,128]{2,1,0:T(8,128)(2,1)} %x_ref.3, f32[1,128]{1,0:T(1,128)} %bitcast.15, f32[1,128]{1,0:T(1,128)} %bitcast.17, bf16[128,512]{1,0:T(8,128)(2,1)} %weights_ref.3), custom_call_target="tpu_custom_call" | custom-call | tf_op jit(solution)/shard_map/prologue/pallas_call | solution.py:82
  4.0 0.0 copy-start.1
  4.0 0.0 copy-start.2
  4.0 0.0 copy-start.6
  4.0 31.1 %all-to-all-start = ((bf16[128,32,128]{2,1,0:T(8,128)(2,1)}), bf16[128,32,128]{2,1,0:T(8,128)(2,1)S(1)}, u32[]{:S(2)}, u32[]{:S(2)}) async-start(bf16[128,32,128]{2,1,0:T(8,128)(2,1)} %prologue.1), calls=%async_computation | async-start | bytes 2097152 | tf_op jit(solution)/shard_map/all_to_all | solution.py:226
  35.1 0.0 copy-start.3
  35.2 0.0 copy-start.4
  35.2 0.0 copy-start.5
  35.2 0.0 copy-done.1
  35.2 0.0 copy-done.2
  35.2 0.0 copy-done.6
  35.2 0.6 copy-done.3
  35.8 0.0 copy-done.4
  35.8 0.0 copy-done.5
  35.8 0.8 output_gates.1
  36.6 49.5 %all-to-all-done = bf16[128,32,128]{2,1,0:T(8,128)(2,1)S(1)} async-done(((bf16[128,32,128]{2,1,0:T(8,128)(2,1)}), bf16[128,32,128]{2,1,0:T(8,128)(2,1)S(1)}, u32[]{:S(2)}, u32[]{:S(2)}) %all-to-all-start) | async-done | bytes 1048608 | tf_op jit(solution)/shard_map/all_to_all | solution.py:226
  86.1 0.8 middle.1
  87.0 42.3 %all_to_all.10 = bf16[128,16,128]{2,1,0:T(8,128)(2,1)S(1)} all-to-all(bf16[128,16,128]{2,1,0:T(8,128)(2,1)S(1)} %bitcast.14), channel_id=1, replica_groups=mesh['groups'=2,'row'=16,'col'=4,'ksplit'=2] {'row','col','ksplit'}, dimensions={0} | all-to-all | bytes 1048576 | tf_op jit(solution)/shard_map/all_to_all | solution.py:228
  129.2 0.1 convert_reduce_fusion
  129.4 0.2 fusion.3
  129.6 0.3 fusion.6
  129.9 0.0 copy-done
  130.0 1.1 fusion
  (2 shorter events, 0.0 us)
Async XLA Ops:
  0.0 129.9 %copy-start = (bf16[128,128]{1,0:T(8,128)(2,1)S(1)}, bf16[128,128]{1,0:T(8,128)(2,1)}, u32[]{:S(2)}) copy-start(bf16[128,128]{1,0:T(8,128)(2,1)} %param.17) | copy-start | bytes 98308
  4.0 31.2 %copy-start.1 = (bf16[32,64,128]{2,1,0:T(8,128)(2,1)S(1)}, bf16[32,64,128]{2,1,0:T(8,128)(2,1)}, u32[]{:S(2)}) copy-start(bf16[32,64,128]{2,1,0:T(8,128)(2,1)} %x_ref.3) | copy-start | bytes 1572868
  4.0 31.2 %copy-start.2 = (bf16[128,128]{1,0:T(8,128)(2,1)S(1)}, bf16[128,128]{1,0:T(8,128)(2,1)}, u32[]{:S(2)}) copy-start(bf16[128,128]{1,0:T(8,128)(2,1)} %weights_ref.2) | copy-start | bytes 98308
  4.0 31.2 %copy-start.6 = (f32[128]{0:T(128)S(1)}, f32[128]{0:T(128)}, u32[]{:S(2)}) copy-start(f32[128]{0:T(128)} %param.16) | copy-start | bytes 1540
  4.0 82.1 %all-to-all-start = ((bf16[128,32,128]{2,1,0:T(8,128)(2,1)}), bf16[128,32,128]{2,1,0:T(8,128)(2,1)S(1)}, u32[]{:S(2)}, u32[]{:S(2)}) async-start(bf16[128,32,128]{2,1,0:T(8,128)(2,1)} %prologue.1), calls=%async_computation | async-start | bytes 2097152 | tf_op jit(solution)/shard_map/all_to_all | solution.py:226
  35.1 0.7 copy-start.3
  35.2 0.7 copy-start.4
  35.2 0.7 copy-start.5
